TPU v7x, 128 devices: a whole 4x4x4 slice. The times are simulated.
128 devices in a mesh: gx: 4 (over y), gy: 32 (over z, x, core).
Axes of the slice: x: 4, y: 4, z: 4, core: 2. Of those that a mesh axis runs over, the one named last changes fastest.
Arguments:
- point_coords: float32 [512, 3, 256], P(('gx', 'gy')), may hold values from -2 to 2
- charge: float32 [512, 256], P(('gx', 'gy')), may hold values from -0.12 to 0.12
- shell_index: int32 [512, 32, 256], P(('gx', 'gy')), may hold values from 0 to 63
- neighbours: int32 [512, 32], P(('gx', 'gy')), may hold values from 0 to 4095, as said below
- neighbour_count: int32 [512], P(('gx', 'gy')), may hold values from 24 to 32
- batch_load: int32 [128], P(('gx', 'gy')), may hold values from 3 to 4, as said below
- atom_coords: float32 [3, 4096], replicated, may hold values from -2 to 2
- owner_slot: int32 [4096], replicated, may hold values from 0 to 4095, as said below
Outputs:
- potential: float32 [512, 256], P(('gx', 'gy'))
- moments: float32 [4096, 3136], P(('gx', 'gy'))
Inputs may be any that keep to these rules, and one draw needn't show every extreme that they name: `neighbours`: atom labels. On every device, at most 1 of its 128 neighbour slots, live or not, name atoms whose owner_slot lies in one block of 32 rows; on every device some block gets exactly 1. `owner_slot`: each row number once. `batch_load`: some device has all 4 slots live.
All inputs are finite; a program needn't handle non-finite values.
Results may differ from a plain program's by a relative error of at most 0.0003.
Values sent between devices are 32-bit elements; how exact they have to be, the bound alone decides.
A program may use at most 64 MiB of HBM per device.

v0:
```python
import math

import jax
import jax.numpy as jnp
from jax import lax
from jax.sharding import PartitionSpec as P

SHELLS = 64


SOFTEN = 0.01
HIGHEST = lax.Precision.HIGHEST


def harmonics(along_x, along_y, along_z):
    cosines = [jnp.ones_like(along_x)]
    sines = [jnp.zeros_like(along_x)]
    for azimuth in range(1, 7):
        previous_cos = cosines[-1]
        previous_sin = sines[-1]
        cosines.append(previous_cos * along_x - previous_sin * along_y)
        sines.append(previous_cos * along_y + previous_sin * along_x)
    legendre = {}
    for azimuth in range(7):
        legendre[azimuth, azimuth] = jnp.ones_like(along_z) * float(
            math.prod(range(1, 2 * azimuth, 2))
        )
        if azimuth < 6:
            legendre[azimuth + 1, azimuth] = (
                (2 * azimuth + 1) * along_z * legendre[azimuth, azimuth]
            )
        for degree in range(azimuth + 2, 7):
            legendre[degree, azimuth] = (
                (2 * degree - 1) * along_z * legendre[degree - 1, azimuth]
                - (degree + azimuth - 1) * legendre[degree - 2, azimuth]
            ) / (degree - azimuth)
    results = []
    for degree in range(7):
        for signed in range(-degree, degree + 1):
            azimuth = abs(signed)
            factor = math.sqrt(
                (2 * degree + 1)
                / (4 * math.pi)
                * math.factorial(degree - azimuth)
                / math.factorial(degree + azimuth)
            )
            if signed == 0:
                results.append(factor * legendre[degree, 0])
            elif signed > 0:
                results.append(
                    math.sqrt(2.0) * factor * legendre[degree, azimuth] * cosines[azimuth]
                )
            else:
                results.append(math.sqrt(2.0) * factor * legendre[degree, azimuth] * sines[azimuth])
    return jnp.stack(results)


def green_table():
    shell_rank = jnp.arange(SHELLS, dtype=jnp.float32)
    radius = 0.5 * jnp.exp(2.3 * shell_rank / SHELLS)
    nearer = jnp.minimum(radius[:, None], radius[None, :])
    farther = jnp.maximum(radius[:, None], radius[None, :])
    kernels = []
    for degree in range(7):
        kernel = 4.0 * math.pi / (2 * degree + 1) * nearer**degree / farther ** (degree + 1)
        kernels.extend([kernel] * (2 * degree + 1))
    return jnp.stack(kernels)


def batch_geometry(coords, atom_place, count):
    offset = coords[:, None, :] - atom_place[:, :, None]
    squared = jnp.sum(offset * offset, axis=0)
    scale = 1.0 / jnp.sqrt(squared + SOFTEN)
    harmonic = harmonics(offset[0] * scale, offset[1] * scale, offset[2] * scale)
    slot_live = jnp.arange(atom_place.shape[1], dtype=jnp.int32) < count
    closeness = jnp.where(slot_live[:, None], 1.0 / (1.0 + squared), 0.0)
    share = closeness / jnp.sum(closeness, axis=0, keepdims=True)
    return (harmonic, share)


def body(
    point_coords,
    charge,
    shell_index,
    neighbours,
    neighbour_count,
    batch_load,
    atom_coords,
    owner_slot,
):
    batches = charge.shape[0]
    slots = neighbours.shape[1]
    count_gx = lax.axis_size("gx")
    count_gy = lax.axis_size("gy")
    devices = count_gx * count_gy
    owned = owner_slot.shape[0] // devices
    spaces = batches * slots
    per_peer = spaces // devices
    slot_rank = jnp.arange(slots, dtype=jnp.int32)
    shell_rank = jnp.arange(SHELLS, dtype=jnp.int32)
    live_batch = (jnp.arange(batches, dtype=jnp.int32) < batch_load[0]).astype(jnp.float32)
    green = green_table()

    def forward(inputs):
        coords, weights_here, shells_here, labels, count, live = inputs
        harmonic, share = batch_geometry(coords, atom_coords[:, labels], count)
        weighted = harmonic * (share * weights_here[None, :] * live)[None]
        selector = (shells_here[:, :, None] == shell_rank).astype(jnp.float32)
        partial_value = jnp.einsum("lip,ips->ils", weighted, selector, precision=HIGHEST)
        return (partial_value, harmonic)

    partial_value, harmonic = lax.map(
        forward, (point_coords, charge, shell_index, neighbours, neighbour_count, live_batch)
    )
    width = partial_value.shape[2] * partial_value.shape[3]
    rows_flat = partial_value.reshape(batches * slots, width)
    target_slot = owner_slot[neighbours.reshape(-1)]
    owner = target_slot // owned
    local = target_slot % owned
    row_live = (
        (slot_rank[None, :] < neighbour_count[:, None]) & (live_batch[:, None] > 0.0)
    ).reshape(-1)
    marks = (
        (owner[:, None] == jnp.arange(devices, dtype=jnp.int32)[None, :]) & row_live[:, None]
    ).astype(jnp.int32)
    before = jnp.cumsum(marks, axis=0) - marks
    place = jnp.sum(before * marks, axis=1)
    target = jnp.where(row_live, owner * per_peer + place, spaces)
    outgoing = jnp.zeros((spaces, width), jnp.float32).at[target].set(rows_flat, mode="drop")
    labels_out = (
        jnp.zeros((spaces,), jnp.float32).at[target].set(local.astype(jnp.float32), mode="drop")
    )
    arrived, arrived_label = (
        lax.all_to_all(outgoing, ("gx", "gy"), split_axis=0, concat_axis=0, tiled=True),
        lax.all_to_all(labels_out, ("gx", "gy"), split_axis=0, concat_axis=0, tiled=True),
    )
    picker = (jnp.arange(owned, dtype=jnp.float32)[:, None] == arrived_label[None, :]).astype(
        jnp.float32
    )
    moments = jnp.dot(picker, arrived, precision=HIGHEST, preferred_element_type=jnp.float32)
    arrived_rows = arrived_label.astype(jnp.int32)
    reply = moments[arrived_rows]
    returned = lax.all_to_all(reply, ("gx", "gy"), split_axis=0, concat_axis=0, tiled=True)
    fetched = returned[jnp.minimum(target, spaces - 1)].reshape(batches, slots, -1, SHELLS)
    fetched = jnp.einsum("lst,bjlt->bjls", green, fetched, precision=HIGHEST)

    def evaluate(inputs):
        table_rows, harmonic_here, shells_here, count, live = inputs
        selector = (shells_here[:, :, None] == shell_rank).astype(jnp.float32)
        picked = jnp.einsum("jls,jps->jlp", table_rows, selector, precision=HIGHEST)
        total = jnp.sum(picked * jnp.transpose(harmonic_here, (1, 0, 2)), axis=1)
        slot_live = slot_rank < count
        return jnp.sum(jnp.where(slot_live[:, None], total, 0.0), axis=0) * live

    potential = lax.map(evaluate, (fetched, harmonic, shell_index, neighbour_count, live_batch))
    return (potential, moments)


def solution(mesh):
    return jax.shard_map(
        body,
        mesh=mesh,
        in_specs=(
            P(("gx", "gy"), None, None),
            P(("gx", "gy"), None),
            P(("gx", "gy"), None, None),
            P(("gx", "gy"), None),
            P(("gx", "gy")),
            P(("gx", "gy")),
            P(),
            P(),
        ),
        out_specs=(P(("gx", "gy"), None), P(("gx", "gy"), None)),
        check_vma=False,
    )
```

profile of v0, /device:TPU:1, one launch (start us, length us, event | category | flops | bytes accessed | tf_op | source)
XLA Modules:
  0.0 196.5 jit_solution(14919243234107487428)
XLA Ops:
  2.3 0.8 reshape.1080
  3.1 1.1 gather_fusion.1
  4.7 1.0 scatter_custom_fusion
  5.7 0.7 copy.58
  6.4 11.5 %all-to-all-start = ((f32[128,1,1]{2,1,0:T(1,128)}), f32[128,1,1]{2,1,0:T(1,128)S(1)}, u32[]{:S(2)}, u32[]{:S(2)}) async-start(f32[128,1,1]{2,1,0:T(1,128)} %copy.58), calls=%async_computation | async-start | bytes 131072 | tf_op jit(solution)/shard_map/all_to_all | solution.py:135
  18.0 2.8 %copy.60 = f32[3,4096]{0,1:T(8,128)} copy(f32[3,4096]{1,0:T(4,128)} %param.18) | data formatting | bytes 98304
  20.8 50.2 %while.28 = (s32[]{:T(128)}, f32[4,32,49,64]{3,2,1,0:T(8,128)}, f32[4,49,32,256]{3,2,1,0:T(8,128)}, f32[4,3,256]{2,0,1:T(4,128)}, s32[4,32]{1,0:T(4,128)}, /*ind...) while((s32[]{:T(128)}, f32[4,32,49,64]{3,2,1,0:T(8,128)}, ...), condition=%wide.region_6.7_spmd.clone, body=%wide.region_3.6_spmd.clone.sunk | while | flops 312320896 | bytes 15035021 | solution.py:112
  21.5 2.2 %gather_fusion = f32[32,3]{1,0:T(8,128)S(1)} fusion(f32[3,4096]{0,1:T(8,128)} %get-tuple-element.713, s32[1024]{0:T(1024)S(1)} %pad_clamp_fusion.5), kind=kCustom, calls=%fused_computation.clone.clone.1 | custom fusion | bytes 896 | tf_op jit(solution)/shard_map/while/body/eval_jaxpr/gather | solution.py:106
  29.1 2.9 %fusion.71 = f32[4,32,49,64]{3,2,1,0:T(8,128)} fusion(f32[4,32,49,64]{3,2,1,0:T(8,128)} %get-tuple-element.698, s32[]{:T(128)S(6)} %copy.162, f32[49,32,256]{2,1,0:T(8,128)S(1)} %broadcast_multiply_fusion.4, s32[32,256]{1,0:T(8,128)S(1)} %dynamic-slice_bitcast_fusion.4), kind=kOutput, calls=%fused_computation.14.clone.1 | convolution fusion | flops 308805632 | bytes 2555908 | tf_op jit(solution)/shard_map/while/body/eval_jaxpr/lip,ips->ils/dot_general | solution.py:109
  32.0 1.3 bitcast_dynamic-update-slice_fusion.2
  34.0 2.2 %gather_fusion = f32[32,3]{1,0:T(8,128)S(1)} fusion(f32[3,4096]{0,1:T(8,128)} %get-tuple-element.713, s32[1024]{0:T(1024)S(1)} %pad_clamp_fusion.5), kind=kCustom, calls=%fused_computation.clone.clone.1 | custom fusion | bytes 896 | tf_op jit(solution)/shard_map/while/body/eval_jaxpr/gather | solution.py:106
  41.7 2.9 %fusion.71 = f32[4,32,49,64]{3,2,1,0:T(8,128)} fusion(f32[4,32,49,64]{3,2,1,0:T(8,128)} %get-tuple-element.698, s32[]{:T(128)S(6)} %copy.162, f32[49,32,256]{2,1,0:T(8,128)S(1)} %broadcast_multiply_fusion.4, s32[32,256]{1,0:T(8,128)S(1)} %dynamic-slice_bitcast_fusion.4), kind=kOutput, calls=%fused_computation.14.clone.1 | convolution fusion | flops 308805632 | bytes 2555908 | tf_op jit(solution)/shard_map/while/body/eval_jaxpr/lip,ips->ils/dot_general | solution.py:109
  44.6 1.3 bitcast_dynamic-update-slice_fusion.2
  46.6 2.2 %gather_fusion = f32[32,3]{1,0:T(8,128)S(1)} fusion(f32[3,4096]{0,1:T(8,128)} %get-tuple-element.713, s32[1024]{0:T(1024)S(1)} %pad_clamp_fusion.5), kind=kCustom, calls=%fused_computation.clone.clone.1 | custom fusion | bytes 896 | tf_op jit(solution)/shard_map/while/body/eval_jaxpr/gather | solution.py:106
  54.2 3.0 %fusion.71 = f32[4,32,49,64]{3,2,1,0:T(8,128)} fusion(f32[4,32,49,64]{3,2,1,0:T(8,128)} %get-tuple-element.698, s32[]{:T(128)S(6)} %copy.162, f32[49,32,256]{2,1,0:T(8,128)S(1)} %broadcast_multiply_fusion.4, s32[32,256]{1,0:T(8,128)S(1)} %dynamic-slice_bitcast_fusion.4), kind=kOutput, calls=%fused_computation.14.clone.1 | convolution fusion | flops 308805632 | bytes 2555908 | tf_op jit(solution)/shard_map/while/body/eval_jaxpr/lip,ips->ils/dot_general | solution.py:109
  57.1 1.3 bitcast_dynamic-update-slice_fusion.2
  59.1 2.2 %gather_fusion = f32[32,3]{1,0:T(8,128)S(1)} fusion(f32[3,4096]{0,1:T(8,128)} %get-tuple-element.713, s32[1024]{0:T(1024)S(1)} %pad_clamp_fusion.5), kind=kCustom, calls=%fused_computation.clone.clone.1 | custom fusion | bytes 896 | tf_op jit(solution)/shard_map/while/body/eval_jaxpr/gather | solution.py:106
  66.7 2.9 %fusion.71 = f32[4,32,49,64]{3,2,1,0:T(8,128)} fusion(f32[4,32,49,64]{3,2,1,0:T(8,128)} %get-tuple-element.698, s32[]{:T(128)S(6)} %copy.162, f32[49,32,256]{2,1,0:T(8,128)S(1)} %broadcast_multiply_fusion.4, s32[32,256]{1,0:T(8,128)S(1)} %dynamic-slice_bitcast_fusion.4), kind=kOutput, calls=%fused_computation.14.clone.1 | convolution fusion | flops 308805632 | bytes 2555908 | tf_op jit(solution)/shard_map/while/body/eval_jaxpr/lip,ips->ils/dot_general | solution.py:109
  69.6 1.3 bitcast_dynamic-update-slice_fusion.2
  74.2 3.9 %reshape.1127 = f32[128,3136]{1,0:T(8,128)} reshape(f32[4,32,49,64]{3,2,1,0:T(8,128)} %get-tuple-element.303) | data formatting | bytes 3211264 | tf_op jit(solution)/shard_map/reshape | solution.py:116
  78.2 2.8 %scatter_custom_fusion.1 = f32[128,3136]{1,0:T(8,128)S(1)} fusion(s32[128]{0:T(128)S(1)} %fusion.56, f32[128,3136]{1,0:T(8,128)} %reshape.1127, f32[]{:T(128)} %constant.486.clone.1), kind=kCustom, calls=%fused_computation.131 | custom fusion | bytes 1606144 | tf_op jit(solution)/shard_map/scatter | solution.py:129
  81.0 2.9 %copy.62 = f32[128,1,3136]{2,1,0:T(1,128)} copy(f32[128,1,3136]{2,0,1:T(8,128)S(1)} %bitcast.124) | data formatting | bytes 3211264 | tf_op jit(solution)/shard_map/all_to_all | solution.py:134
  83.8 9.8 %all-to-all-start.1 = ((f32[128,1,3136]{2,1,0:T(1,128)}), f32[128,1,3136]{2,1,0:T(1,128)S(1)}, u32[]{:S(2)}, u32[]{:S(2)}) async-start(f32[128,1,3136]{2,1,0:T(1,128)} %copy.62), calls=%async_computation.1 | async-start | bytes 3276800 | tf_op jit(solution)/shard_map/all_to_all | solution.py:134
  94.2 1.0 reduce
  95.2 2.4 %convert_reduce_fusion = s32[128]{0:T(128)S(1)} fusion(f32[128,1,1]{2,1,0:T(1,128)S(1)} %all-to-all-done), kind=kLoop, calls=%fused_computation.196 | loop fusion | flops 128 | bytes 1024 | tf_op jit(solution)/shard_map/convert_element_type | solution.py:141
  97.6 21.6 %all-to-all-done.1 = f32[128,1,3136]{2,1,0:T(1,128)S(1)} async-done(((f32[128,1,3136]{2,1,0:T(1,128)}), f32[128,1,3136]{2,1,0:T(1,128)S(1)}, u32[]{:S(2)}, u32[]{:S(2)}) %all-to-all-start.1) | async-done | bytes 1605664 | tf_op jit(solution)/shard_map/all_to_all | solution.py:134
  119.1 1.6 copy.63
  120.8 0.9 fusion.30
  121.7 1.2 gather_fusion.2
  123.0 2.9 %copy.64 = f32[128,1,3136]{2,1,0:T(1,128)} copy(f32[128,1,3136]{2,0,1:T(8,128)S(1)} %bitcast.125) | data formatting | bytes 3211264 | tf_op jit(solution)/shard_map/all_to_all | solution.py:143
  125.9 4.4 %all-to-all-start.2 = ((f32[128,1,3136]{2,1,0:T(1,128)}), f32[128,1,3136]{2,1,0:T(1,128)S(1)}, u32[]{:S(2)}, u32[]{:S(2)}) async-start(f32[128,1,3136]{2,1,0:T(1,128)} %copy.64), calls=%async_computation.2 | async-start | bytes 3276800 | tf_op jit(solution)/shard_map/all_to_all | solution.py:143
  135.2 20.8 %all-to-all-done.2 = f32[128,1,3136]{2,1,0:T(1,128)S(1)} async-done(((f32[128,1,3136]{2,1,0:T(1,128)}), f32[128,1,3136]{2,1,0:T(1,128)S(1)}, u32[]{:S(2)}, u32[]{:S(2)}) %all-to-all-start.2) | async-done | bytes 1605664 | tf_op jit(solution)/shard_map/all_to_all | solution.py:143
  156.1 1.2 gather_fusion.3
  157.3 2.2 %reshape.1082 = f32[4,32,49,64]{3,2,1,0:T(8,128)} reshape(f32[128,3136]{1,0:T(8,128)S(1)} %gather_fusion.3) | data formatting | bytes 3211264 | tf_op jit(solution)/shard_map/reshape | solution.py:144
  159.5 5.8 %fusion.26 = f32[4,32,49,64]{3,1,0,2:T(8,128)S(1)} fusion(f32[4,32,49,64]{3,2,1,0:T(8,128)} %reshape.1082, f32[49,64,64]{2,1,0:T(8,128)} %constant_dynamic-update-slice_fusion.49), kind=kOutput, calls=%fused_computation.126 | convolution fusion | flops 308281344 | bytes 4014080 | tf_op jit(solution)/shard_map/lst,bjlt->bjls/dot_general | solution.py:145
  165.4 31.2 %while.29 = (s32[]{:T(128)}, f32[4,256]{1,0:T(4,128)}, s32[4]{0:T(128)S(1)}, f32[4,32,49,64]{3,1,0,2:T(8,128)S(1)}, s32[4,32,256]{2,1,0:T(8,128)S(1)}, /*index=5...) while((s32[]{:T(128)}, f32[4,256]{1,0:T(4,128)}, s32[4]{0:T(128)S(1)}, ...), condition=%wide.region_11.12_spmd.clone, body=%wide.region_8.11_spmd.clone.sunk | while | flops 309616672 | bytes 6190293 | solution.py:155
  165.4 1.5 constant_dynamic-slice_fusion.11
  167.0 2.3 %fusion.72 = f32[32,256]{1,0:T(8,128)S(1)} fusion(f32[1,49,32,256]{3,2,1,0:T(8,128)S(1)} %constant_dynamic-slice_fusion.11, s32[32,256]{1,0:T(8,128)S(1)} %dynamic-slice_bitcast_fusion.5, f32[1,32,49,64]{3,1,0,2:T(8,128)S(1)} %constant_dynamic-slice_fusion.12), kind=kOutput, calls=%fused_computation.115.clone.1 | convolution fusion | flops 309600256 | bytes 2072576 | tf_op jit(solution)/shard_map/while/body/eval_jaxpr/jls,jps->jlp/dot_general | solution.py:150
  171.9 1.3 dynamic_update_slice.34
  173.2 1.5 constant_dynamic-slice_fusion.11
  174.8 2.3 %fusion.72 = f32[32,256]{1,0:T(8,128)S(1)} fusion(f32[1,49,32,256]{3,2,1,0:T(8,128)S(1)} %constant_dynamic-slice_fusion.11, s32[32,256]{1,0:T(8,128)S(1)} %dynamic-slice_bitcast_fusion.5, f32[1,32,49,64]{3,1,0,2:T(8,128)S(1)} %constant_dynamic-slice_fusion.12), kind=kOutput, calls=%fused_computation.115.clone.1 | convolution fusion | flops 309600256 | bytes 2072576 | tf_op jit(solution)/shard_map/while/body/eval_jaxpr/jls,jps->jlp/dot_general | solution.py:150
  179.7 1.3 dynamic_update_slice.34
  181.0 1.5 constant_dynamic-slice_fusion.11
  182.6 2.3 %fusion.72 = f32[32,256]{1,0:T(8,128)S(1)} fusion(f32[1,49,32,256]{3,2,1,0:T(8,128)S(1)} %constant_dynamic-slice_fusion.11, s32[32,256]{1,0:T(8,128)S(1)} %dynamic-slice_bitcast_fusion.5, f32[1,32,49,64]{3,1,0,2:T(8,128)S(1)} %constant_dynamic-slice_fusion.12), kind=kOutput, calls=%fused_computation.115.clone.1 | convolution fusion | flops 309600256 | bytes 2072576 | tf_op jit(solution)/shard_map/while/body/eval_jaxpr/jls,jps->jlp/dot_general | solution.py:150
  187.5 1.3 dynamic_update_slice.34
  188.8 1.5 constant_dynamic-slice_fusion.11
  190.4 2.3 %fusion.72 = f32[32,256]{1,0:T(8,128)S(1)} fusion(f32[1,49,32,256]{3,2,1,0:T(8,128)S(1)} %constant_dynamic-slice_fusion.11, s32[32,256]{1,0:T(8,128)S(1)} %dynamic-slice_bitcast_fusion.5, f32[1,32,49,64]{3,1,0,2:T(8,128)S(1)} %constant_dynamic-slice_fusion.12), kind=kOutput, calls=%fused_computation.115.clone.1 | convolution fusion | flops 309600256 | bytes 2072576 | tf_op jit(solution)/shard_map/while/body/eval_jaxpr/jls,jps->jlp/dot_general | solution.py:150
  195.2 1.3 dynamic_update_slice.34
  (360 shorter events, 43.5 us)
Async XLA Ops:
  0.6 2.4 %copy-start = (s32[4096]{0:T(1024)S(1)}, s32[4096]{0:T(1024)}, u32[]{:S(2)}) copy-start(s32[4096]{0:T(1024)} %param.19) | copy-start | bytes 49156
  0.6 20.1 %copy-start.4 = (s32[4]{0:T(128)S(1)}, s32[4]{0:T(128)}, u32[]{:S(2)}) copy-start(s32[4]{0:T(128)} %param.16) | copy-start | bytes 52
  0.7 20.1 %copy-start.3 = (s32[4,32,256]{2,1,0:T(8,128)S(1)}, s32[4,32,256]{2,1,0:T(8,128)}, u32[]{:S(2)}) copy-start(s32[4,32,256]{2,1,0:T(8,128)} %param.14) | copy-start | bytes 393220
  6.4 77.4 %all-to-all-start = ((f32[128,1,1]{2,1,0:T(1,128)}), f32[128,1,1]{2,1,0:T(1,128)S(1)}, u32[]{:S(2)}, u32[]{:S(2)}) async-start(f32[128,1,1]{2,1,0:T(1,128)} %copy.58), calls=%async_computation | async-start | bytes 131072 | tf_op jit(solution)/shard_map/all_to_all | solution.py:135
  83.8 35.3 %all-to-all-start.1 = ((f32[128,1,3136]{2,1,0:T(1,128)}), f32[128,1,3136]{2,1,0:T(1,128)S(1)}, u32[]{:S(2)}, u32[]{:S(2)}) async-start(f32[128,1,3136]{2,1,0:T(1,128)} %copy.62), calls=%async_computation.1 | async-start | bytes 3276800 | tf_op jit(solution)/shard_map/all_to_all | solution.py:134
  94.2 3.4 %copy-start.2 = (f32[49,64,64]{2,1,0:T(8,128)}, f32[49,64,64]{2,1,0:T(8,128)S(1)}, u32[]{:S(2)}) copy-start(f32[49,64,64]{2,1,0:T(8,128)S(1)} %constant_dynamic-update-slice_fusion.56) | copy-start | bytes 2408452
  121.7 1.3 copy-start.1
  125.9 30.1 %all-to-all-start.2 = ((f32[128,1,3136]{2,1,0:T(1,128)}), f32[128,1,3136]{2,1,0:T(1,128)S(1)}, u32[]{:S(2)}, u32[]{:S(2)}) async-start(f32[128,1,3136]{2,1,0:T(1,128)} %copy.64), calls=%async_computation.2 | async-start | bytes 3276800 | tf_op jit(solution)/shard_map/all_to_all | solution.py:143
where the time goes:
time: 198 us; the launch traced here: 197 us
  local copies, waits for them, and re-layouts  66.7 us (34%)
  waiting for transfers between devices  42.3 us (21%)
  other arithmetic  30.6 us (15%)
  matrix products  27.8 us (14%)
  starting transfers between devices  25.7 us (13%)
    all_to_all x1, waiting for transfers between devices, body(): lax.all_to_all(outgoing, ('gx', 'gy'), split_axis=0, concat_axis=0, tiled...  21.6 us
    all_to_all x1, waiting for transfers between devices, body(): lax.all_to_all(reply, ('gx', 'gy'), split_axis=0, concat_axis=0, tiled=True)  20.8 us
    dynamic_slice x28, local copies, waits for them, and re-layouts, body(): lax.map(forward, (point_coords, charge, shell_index, neighbours, neighbou...  15.3 us
    dot_general x4, matrix products, forward(): jnp.einsum('lip,ips->ils', weighted, selector, precision=HIGHEST)  11.8 us
    all_to_all x1, starting transfers between devices, body(): lax.all_to_all(labels_out, ('gx', 'gy'), split_axis=0, concat_axis=0, til...  11.5 us
    all_to_all x1, starting transfers between devices, body(): lax.all_to_all(outgoing, ('gx', 'gy'), split_axis=0, concat_axis=0, tiled...  9.77 us
    dot_general x4, matrix products, evaluate(): picked = jnp.einsum('jls,jps->jlp', table_rows, selector, precision=HIGHEST)  9.26 us
    gather x8, local copies, waits for them, and re-layouts, forward(): harmonic, share = batch_geometry(coords, atom_coords[:, labels], count)  8.97 us
  transfers between devices with their start and end apart: 3, of which 2 were waited for; matrix products, arithmetic and copies ran while one was open for 37% of the time, Pallas kernels for 0%

commit v1 on v0

v1 whole, which is shorter than its diff:
```python
import functools
import math

import jax
import jax.numpy as jnp
import numpy as np
from jax import lax
from jax.experimental import pallas as pl
from jax.experimental.pallas import tpu as pltpu
from jax.sharding import PartitionSpec as P

MESH = pl.DeviceIdType.MESH
F32 = jnp.float32
BF16 = jnp.bfloat16
SHELLS = 64
LMAX = 6
LM = 49
KP = 56
SOFTEN = 0.01
ROWS = 11
PITCH = 16
SLOTP = 136


def green_pair():
    rank = np.arange(SHELLS, dtype=np.float64)
    radius = 0.5 * np.exp(2.3 * rank / SHELLS)
    nearer = np.minimum(radius[:, None], radius[None, :])
    farther = np.maximum(radius[:, None], radius[None, :])
    full = np.stack(
        [
            4.0 * math.pi / (2 * d + 1) * nearer**d / farther ** (d + 1)
            for d in range(LMAX + 1)
        ]
    )
    full = np.concatenate([full, full], axis=2).astype(np.float32)
    high = full.astype(jnp.bfloat16)
    low = (full - high.astype(np.float32)).astype(jnp.bfloat16)
    return high, low


def split(x):
    high = x.astype(BF16).astype(F32)
    return high, x - high


def dot(a, b, dims=((1,), (0,))):
    return lax.dot_general(a, b, (dims, ((), ())), preferred_element_type=F32)


def harmonics(ux, uy, uz):
    cosine = [None]
    sine = [None]
    for m in range(1, LMAX + 1):
        if m == 1:
            cosine.append(ux)
            sine.append(uy)
        else:
            pc, ps = cosine[-1], sine[-1]
            cosine.append(pc * ux - ps * uy)
            sine.append(pc * uy + ps * ux)

    def norm(d, m):
        value = math.sqrt(
            (2 * d + 1) / (4 * math.pi) * math.factorial(d - m) / math.factorial(d + m)
        )
        return value * (math.sqrt(2.0) if m else 1.0)

    out = {}
    for m in range(LMAX + 1):
        start = norm(m, m) * float(math.prod(range(1, 2 * m, 2)))
        older, old = None, None
        for d in range(m, LMAX + 1):
            if d == m:
                now = start
            elif d == m + 1:
                now = uz * ((2 * m + 1) * start * norm(d, m) / norm(m, m))
            else:
                ca = (2 * d - 1) / (d - m) * norm(d, m) / norm(d - 1, m)
                cb = (d + m - 1) / (d - m) * norm(d, m) / norm(d - 2, m)
                now = (ca * uz) * old - cb * older
            if m == 0:
                out[d * d + d] = now if d else jnp.full(ux.shape, start, F32)
            else:
                out[d * d + d + m] = cosine[m] * now
                out[d * d + d - m] = sine[m] * now
            older, old = old, now
    return out


def pack_kernel(
    labels, count, load, owner, atoms, coords, charge, shell, pay, meta, place, src
):
    batches, slots = labels.shape
    spaces = batches * slots
    devices = pay.shape[0]
    owned = owner.shape[0] // devices

    for b in range(batches):

        @pl.loop(0, slots, unroll=4)
        def _(s):
            label = labels[b, s]
            target = owner[label]
            row = b * slots + s
            for c in range(3):
                place[c, pl.ds(row, 1), :] = jnp.full((1, 128), atoms[c, label], F32)
            place[3, pl.ds(row, 1), :] = jnp.full(
                (1, 128), (target // owned).astype(F32), F32
            )
            src[10, pl.ds(row, 1), :] = jnp.full(
                (1, 128), (target % owned).astype(F32), F32
            )

    slot_rank = lax.broadcasted_iota(jnp.int32, (slots, 128), 0)
    lane = lax.broadcasted_iota(jnp.int32, (slots, 128), 1)
    lives = []
    for b in range(batches):
        live = jnp.where(b < load[0], 1.0, 0.0).astype(F32)
        slot_live = slot_rank < count[b]
        here = slice(b * slots, (b + 1) * slots)
        lives.append(jnp.where(slot_live & (lane == b), live, 0.0))
        for h in range(2):
            points = slice(h * 128, (h + 1) * 128)
            squared = 0.0
            for c in range(3):
                offset = coords[b, c : c + 1, points] - place[c, here, :]
                src[2 * c + h, here, :] = offset
                squared = squared + offset * offset
            closeness = jnp.where(slot_live, 1.0 / (1.0 + squared), 0.0)
            total = jnp.sum(closeness, axis=0, keepdims=True)
            scaled = charge[b : b + 1, points] * live / total
            src[6 + h, here, :] = shell[b, :, points].astype(F32)
            src[8 + h, here, :] = jnp.where(slot_live, scaled, 0.0)

    goes = (
        place[3] == lax.broadcasted_iota(jnp.int32, (spaces, devices), 1).astype(F32)
    ).astype(F32)
    goes = goes.T.astype(BF16)
    flat = pay.reshape(devices * PITCH, 128)
    for r in range(ROWS):
        block = src[r]
        high, rest = split(block)
        if r in (6, 7, 10):
            moved = dot(goes, high.astype(BF16))
        else:
            middle, low = split(rest)
            moved = (
                dot(goes, high.astype(BF16))
                + dot(goes, middle.astype(BF16))
                + dot(goes, low.astype(BF16))
            )
        flat[pl.ds(r, devices, stride=PITCH), :] = moved
    meta[...] = dot(goes, jnp.concatenate(lives, axis=0).astype(BF16))


def place_of():
    gx, gy = lax.axis_size("gx"), lax.axis_size("gy")
    me = lax.axis_index("gx") * gy + lax.axis_index("gy")
    return me, gx * gy, gy


def barrier_all(me, devices, gy):
    barrier = pltpu.get_barrier_semaphore()

    @pl.loop(1, devices)
    def _(i):
        peer = lax.rem(me + i, devices)
        pl.semaphore_signal(
            barrier, inc=1, device_id=(peer // gy, lax.rem(peer, gy)), device_id_type=MESH
        )

    pl.semaphore_wait(barrier, devices - 1)


def send_all(me, devices, gy, source, target, send_sem, recv_sem):
    @pl.loop(1, devices)
    def _(i):
        peer = lax.rem(me + i, devices)
        pltpu.make_async_remote_copy(
            src_ref=source(peer),
            dst_ref=target(me),
            send_sem=send_sem,
            recv_sem=recv_sem,
            device_id=(peer // gy, lax.rem(peer, gy)),
            device_id_type=MESH,
        ).start()


def exchange_kernel(rows, pay, arrived, send_sem, recv_sem):
    me, devices, gy = place_of()
    barrier_all(me, devices, gy)
    send_all(
        me,
        devices,
        gy,
        lambda i: pay.at[i, pl.ds(0, rows)],
        lambda i: arrived.at[i, pl.ds(0, rows)],
        send_sem,
        recv_sem,
    )
    arrived[me] = pay[me]
    every = pltpu.make_async_remote_copy(
        src_ref=pay.at[pl.ds(0, devices - 1), pl.ds(0, rows)],
        dst_ref=arrived.at[pl.ds(0, devices - 1), pl.ds(0, rows)],
        send_sem=send_sem,
        recv_sem=recv_sem,
        device_id=(0, 0),
        device_id_type=MESH,
    )
    every.wait_send()
    every.wait_recv()


def owner_kernel(arrived, ghigh, glow, moments, reply, ys, ws, hots, parts, acc, tables):
    sources = arrived.shape[0]
    owned = moments.shape[0]
    flat = arrived.reshape(sources * PITCH, 128)
    groups = sources // 8

    @pl.loop(0, groups)
    def _(g):
        for h in range(2):

            def row(r):
                return flat[pl.ds(g * 8 * PITCH + 2 * r + h, 8, stride=PITCH), :]

            dx, dy, dz = row(0), row(1), row(2)
            squared = dx * dx + dy * dy + dz * dz
            scale = lax.rsqrt(squared + SOFTEN)
            ws[h, pl.ds(pl.multiple_of(g * 8, 8), 8), :] = row(4) / (1.0 + squared)
            values = harmonics(dx * scale, dy * scale, dz * scale)
            for k in range(KP):
                value = values[k] if k < LM else jnp.zeros_like(dx)
                ys[h, pl.ds(g * 8 * KP + k, 8, stride=KP), :] = value

    shell_rank = lax.broadcasted_iota(jnp.int32, (SHELLS, 128), 0).astype(F32)

    def forward(i):
        stack, hot = [], []
        for h in range(2):
            y = ys[h, pl.ds(pl.multiple_of(i * KP, 8), KP), :]
            weighted = y * ws[h, pl.ds(i, 1), :]
            high, low = split(weighted)
            stack.append(jnp.concatenate([high, low], axis=0).astype(BF16))
            shells = flat[pl.ds(i * PITCH + 6 + h, 1), :]
            hot.append((shells == shell_rank).astype(F32).astype(BF16))
        hot = jnp.concatenate(hot, axis=1)
        hots[i] = hot
        both = dot(jnp.concatenate(stack, axis=1), hot, ((1,), (1,)))
        parts[pl.ds(i, KP, stride=SLOTP), :SHELLS] = both[:KP] + both[KP:]

    @pl.loop(0, sources // 4)
    def _(q):
        for e in range(4):
            forward(q * 4 + e)

    marks = flat[pl.ds(10, sources, stride=PITCH), :]
    picks = (
        marks == lax.broadcasted_iota(jnp.int32, (sources, 128), 1).astype(F32)
    ).astype(F32)
    gather = picks[:, :owned].astype(BF16)
    combine = picks.T[:owned].astype(BF16)
    combine = jnp.concatenate([combine, combine], axis=1)

    def summed(k):
        part = parts[pl.ds(k * SLOTP, sources), :SHELLS]
        high, low = split(part)
        both = jnp.concatenate([high, low], axis=0).astype(BF16)
        return dot(combine, both)

    for k in range(0, LM, 2):
        first = summed(k)
        acc[k * owned : (k + 1) * owned, :SHELLS] = first
        if k + 1 < LM:
            second = summed(k + 1)
            acc[(k + 1) * owned : (k + 2) * owned, :SHELLS] = second
            moments[:, k * SHELLS : (k + 2) * SHELLS] = jnp.concatenate(
                [first, second], axis=1
            )
        else:
            moments[:, k * SHELLS : (k + 1) * SHELLS] = first

    for d in range(LMAX + 1):
        begin, end = d * d, (d + 1) * (d + 1)
        high, low = split(acc[begin * owned : end * owned, :SHELLS])
        high, low = high.astype(BF16), low.astype(BF16)
        table = dot(high, ghigh[d]) + dot(low, ghigh[d]) + dot(high, glow[d])
        thigh, tlow = split(table)
        lane = lax.broadcasted_iota(jnp.int32, table.shape, 1)
        table = jnp.where(lane < SHELLS, thigh, tlow).astype(BF16)
        for k in range(begin, end):
            tables[k * SLOTP : k * SLOTP + sources, :] = dot(
                gather, table[(k - begin) * owned : (k - begin + 1) * owned]
            )
    for k in range(LM, KP):
        tables[k * SLOTP : k * SLOTP + sources, :] = jnp.zeros((sources, 128), F32)

    def evaluate(i):
        table = tables[pl.ds(i, KP, stride=SLOTP), :].astype(BF16)
        hot = hots[i]
        picked = dot(table, jnp.concatenate([hot, hot], axis=0))
        for h in range(2):
            y = ys[h, pl.ds(pl.multiple_of(i * KP, 8), KP), :]
            total = jnp.sum(
                picked[:, h * 128 : (h + 1) * 128] * y, axis=0, keepdims=True
            )
            reply[pl.ds(i, 1), h, :] = total

    @pl.loop(0, sources // 4)
    def _(q):
        for e in range(4):
            evaluate(q * 4 + e)


def return_kernel(reply, meta, potential, back, send_sem, recv_sem):
    me, devices, gy = place_of()
    barrier_all(me, devices, gy)
    send_all(
        me,
        devices,
        gy,
        lambda i: reply.at[i],
        lambda i: back.at[i],
        send_sem,
        recv_sem,
    )
    back[me] = reply[me]
    every = pltpu.make_async_remote_copy(
        src_ref=reply.at[pl.ds(0, devices - 1)],
        dst_ref=back.at[pl.ds(0, devices - 1)],
        send_sem=send_sem,
        recv_sem=recv_sem,
        device_id=(0, 0),
        device_id_type=MESH,
    )
    every.wait_send()
    every.wait_recv()
    batches = potential.shape[0]
    mine = meta[...].T[: max(batches, 8)].astype(BF16)
    for h in range(2):
        high, rest = split(back[:, h, :])
        middle, low = split(rest)
        total = (
            dot(mine, high.astype(BF16))
            + dot(mine, middle.astype(BF16))
            + dot(mine, low.astype(BF16))
        )
        potential[:, h * 128 : (h + 1) * 128] = total[:batches]


VMEM = pl.BlockSpec(memory_space=pltpu.VMEM)
SMEM = pl.BlockSpec(memory_space=pltpu.SMEM)


def body(
    point_coords,
    charge,
    shell_index,
    neighbours,
    neighbour_count,
    batch_load,
    atom_coords,
    owner_slot,
):
    batches = charge.shape[0]
    slots = neighbours.shape[1]
    devices = lax.axis_size("gx") * lax.axis_size("gy")
    owned = owner_slot.shape[0] // devices
    spaces = batches * slots
    sds = jax.ShapeDtypeStruct
    pay, meta = pl.pallas_call(
        pack_kernel,
        out_shape=(sds((devices, PITCH, 128), F32), sds((devices, 128), F32)),
        in_specs=[SMEM] * 5 + [VMEM] * 3,
        out_specs=(VMEM, VMEM),
        scratch_shapes=[
            pltpu.VMEM((4, spaces, 128), F32),
            pltpu.VMEM((ROWS, spaces, 128), F32),
        ],
        name="pack",
    )(
        neighbours,
        neighbour_count,
        batch_load,
        owner_slot,
        atom_coords,
        point_coords,
        charge,
        shell_index,
    )
    arrived = pl.pallas_call(
        functools.partial(exchange_kernel, ROWS),
        out_shape=sds((devices, PITCH, 128), F32),
        in_specs=[VMEM],
        out_specs=VMEM,
        scratch_shapes=[pltpu.SemaphoreType.DMA, pltpu.SemaphoreType.DMA],
        compiler_params=pltpu.CompilerParams(collective_id=0, has_side_effects=True),
        name="exchange",
    )(pay)
    ghigh, glow = green_pair()
    moments, reply = pl.pallas_call(
        owner_kernel,
        out_shape=(sds((owned, LM * SHELLS), F32), sds((devices, 2, 128), F32)),
        in_specs=[VMEM] * 3,
        out_specs=(VMEM, VMEM),
        scratch_shapes=[
            pltpu.VMEM((2, devices * KP, 128), F32),
            pltpu.VMEM((2, devices, 128), F32),
            pltpu.VMEM((devices, SHELLS, 256), BF16),
            pltpu.VMEM((KP * SLOTP, 128), F32),
            pltpu.VMEM((LM * owned, 128), F32),
            pltpu.VMEM((KP * SLOTP, 128), F32),
        ],
        name="owner",
    )(arrived, jnp.asarray(ghigh), jnp.asarray(glow))
    potential = pl.pallas_call(
        return_kernel,
        out_shape=sds(charge.shape, F32),
        in_specs=[VMEM, VMEM],
        out_specs=VMEM,
        scratch_shapes=[
            pltpu.VMEM((devices, 2, 128), F32),
            pltpu.SemaphoreType.DMA,
            pltpu.SemaphoreType.DMA,
        ],
        compiler_params=pltpu.CompilerParams(collective_id=1, has_side_effects=True),
        name="giveback",
    )(reply, meta)
    return (potential, moments)


def solution(mesh):
    return jax.shard_map(
        body,
        mesh=mesh,
        in_specs=(
            P(("gx", "gy"), None, None),
            P(("gx", "gy"), None),
            P(("gx", "gy"), None, None),
            P(("gx", "gy"), None),
            P(("gx", "gy")),
            P(("gx", "gy")),
            P(),
            P(),
        ),
        out_specs=(P(("gx", "gy"), None), P(("gx", "gy"), None)),
        check_vma=False,
    )
```

time: 198 us -> 67.7 us (0.34)
  local copies, waits for them, and re-layouts: 66.7 us -> 2.58 us
  Pallas kernels: 0 us -> 63.5 us
  waiting for transfers between devices: 42.3 us -> 0 us
  other arithmetic: 30.6 us -> 0 us
  matrix products: 27.8 us -> 0 us
  starting transfers between devices: 25.7 us -> 0 us
    pallas_call x0 -> x4, Pallas kernels: none -> 63.5 us  [the longest x1 24.7 us: body(): pl.pallas_call(functools.partial(exchange_kernel, ROWS), out_shape=sds((d...]
    all_to_all x3 -> x0, waiting for transfers between devices: 42.3 us -> none  [the longest x1 21.6 us: body(): lax.all_to_all(outgoing, ('gx', 'gy'), split_axis=0, concat_axis=0, tiled...]
    dot_general x10 -> x0, matrix products: 27.8 us -> none  [the longest x4 11.8 us: forward(): jnp.einsum('lip,ips->ils', weighted, selector, precision=HIGHEST)]
    all_to_all x3 -> x0, starting transfers between devices: 25.7 us -> none  [the longest x1 11.5 us: body(): lax.all_to_all(labels_out, ('gx', 'gy'), split_axis=0, concat_axis=0, til...]
    dynamic_slice x36 -> x0, local copies, waits for them, and re-layouts: 21.7 us -> none  [the longest x28 15.3 us: body(): lax.map(forward, (point_coords, charge, shell_index, neighbours, neighbou...]
    gather x11 -> x0, local copies, waits for them, and re-layouts: 12.6 us -> none  [the longest x8 8.97 us: forward(): harmonic, share = batch_geometry(coords, atom_coords[:, labels], count)]
    dynamic_update_slice x8 -> x0, local copies, waits for them, and re-layouts: 10.4 us -> none  [the longest x4 5.22 us: body(): lax.map(evaluate, (fetched, harmonic, shell_index, neighbour_count, live_...]
    all_to_all x5 -> x0, local copies, waits for them, and re-layouts: 8.18 us -> none  [the longest x2 4.48 us: body(): lax.all_to_all(outgoing, ('gx', 'gy'), split_axis=0, concat_axis=0, tiled...]
  transfers between devices with their start and end apart: 3 -> 0, of which waited for: 2 -> 0; matrix products, arithmetic and copies ran while one was open for 37% -> 0% of each run, Pallas kernels for 0% -> 0%
where the time goes in v1:
time: 67.7 us; the launch traced here: 67.4 us
  Pallas kernels  63.5 us (94%)
  local copies, waits for them, and re-layouts  2.58 us (4%)
  between operations  1.29 us (2%)
    pallas_call x1, Pallas kernels, body(): pl.pallas_call(functools.partial(exchange_kernel, ROWS), out_shape=sds((d...  24.7 us
    pallas_call x1, Pallas kernels, body(): pl.pallas_call(owner_kernel, out_shape=(sds((owned, LM * SHELLS), F32), s...  18.9 us
    pallas_call x1, Pallas kernels, body(): pl.pallas_call(return_kernel, out_shape=sds(charge.shape, F32), in_specs=...  14.7 us
    pallas_call x1, Pallas kernels, body(): pl.pallas_call(pack_kernel, out_shape=(sds((devices, PITCH, 128), F32), s...  5.25 us
    unnamed x2, local copies, waits for them, and re-layouts  2.58 us

profile of v1, /device:TPU:1, one launch (start us, length us, event | category | flops | bytes accessed | tf_op | source)
XLA Modules:
  0.0 67.4 jit_solution(10362907900855182608)
XLA Ops:
  1.3 1.3 %copy.12.coords = f32[4,3,256]{2,1,0:T(4,128)} copy(f32[4,3,256]{2,0,1:T(4,128)} %param.10) | data formatting | bytes 24576 | tf_op args[0]
  2.6 5.2 %pack.1 = (f32[128,16,128]{2,1,0:T(8,128)}, f32[128,128]{1,0:T(8,128)}) custom-call(s32[4,32]{1,0:T(4,128)} %labels.1, s32[4]{0:T(128)} %count.1, s32[1]{0:T(128)S(6)} %copy.14.load, s32[4096]{0:T(1024)} %owner.2, f32[3,4096]{1,0:T(4,128)} %atoms.1, f32[4,3,256]{2,1,0:T(4,128)} %copy.12.coords, f32[4,256]{1,0:T(4,128)} %charge.1, s32[4,32,256]{2,1,0:T(8,128)} %shell.1), custom_call_target="tpu_custom_call" | custom-call | tf_op jit(solution)/shard_map/pack/pallas_call | solution.py:372
  7.8 24.7 %exchange.1.arrived = f32[128,16,128]{2,1,0:T(8,128)} custom-call(f32[128,16,128]{2,1,0:T(8,128)} %get-tuple-element.6.pay), custom_call_target="tpu_custom_call" | custom-call | tf_op jit(solution)/shard_map/exchange/pallas_call | solution.py:392
  32.5 18.9 %owner.3 = (f32[32,3136]{1,0:T(8,128)}, f32[128,2,128]{2,1,0:T(2,128)}) custom-call(f32[128,16,128]{2,1,0:T(8,128)} %exchange.1.arrived, bf16[7,64,128]{2,1,0:T(8,128)(2,1)} %constant.4.clone.ghigh, bf16[7,64,128]{2,1,0:T(8,128)(2,1)} %constant.5.clone.glow), custom_call_target="tpu_custom_call" | custom-call | tf_op jit(solution)/shard_map/owner/pallas_call | solution.py:402
  51.4 14.7 %giveback.1 = f32[4,256]{1,0:T(4,128)} custom-call(f32[128,2,128]{2,1,0:T(2,128)} %get-tuple-element.7.reply, f32[128,128]{1,0:T(8,128)} %get-tuple-element.8.meta), custom_call_target="tpu_custom_call" | custom-call | tf_op jit(solution)/shard_map/giveback/pallas_call | solution.py:417
  66.1 1.3 %copy.15 = f32[4,256]{1,0:T(4,128)} copy(f32[4,256]{1,0:T(4,128)} %giveback.1) | data formatting | bytes 8192

commit v2 on v1

v2 whole, which is shorter than its diff:
```python
import math

import jax
import jax.numpy as jnp
import numpy as np
from jax import lax
from jax.experimental import pallas as pl
from jax.experimental.pallas import tpu as pltpu
from jax.sharding import PartitionSpec as P

MESH = pl.DeviceIdType.MESH
F32 = jnp.float32
BF16 = jnp.bfloat16
SHELLS = 64
LMAX = 6
LM = 49
KP = 56
SOFTEN = 0.01
ROWS = 11
PITCH = 16
SLOTP = 136
GROUPS = 8
WAVE = 16


def green_pair():
    rank = np.arange(SHELLS, dtype=np.float64)
    radius = 0.5 * np.exp(2.3 * rank / SHELLS)
    nearer = np.minimum(radius[:, None], radius[None, :])
    farther = np.maximum(radius[:, None], radius[None, :])
    full = np.stack(
        [
            4.0 * math.pi / (2 * d + 1) * nearer**d / farther ** (d + 1)
            for d in range(LMAX + 1)
        ]
    )
    full = np.concatenate([full, full], axis=2).astype(np.float32)
    high = full.astype(jnp.bfloat16)
    low = (full - high.astype(np.float32)).astype(jnp.bfloat16)
    return high, low


def split(x):
    high = x.astype(BF16).astype(F32)
    return high, x - high


def dot(a, b, dims=((1,), (0,))):
    return lax.dot_general(a, b, (dims, ((), ())), preferred_element_type=F32)


def harmonics(ux, uy, uz):
    cosine = [None]
    sine = [None]
    for m in range(1, LMAX + 1):
        if m == 1:
            cosine.append(ux)
            sine.append(uy)
        else:
            pc, ps = cosine[-1], sine[-1]
            cosine.append(pc * ux - ps * uy)
            sine.append(pc * uy + ps * ux)

    def norm(d, m):
        value = math.sqrt(
            (2 * d + 1) / (4 * math.pi) * math.factorial(d - m) / math.factorial(d + m)
        )
        return value * (math.sqrt(2.0) if m else 1.0)

    out = {}
    for m in range(LMAX + 1):
        start = norm(m, m) * float(math.prod(range(1, 2 * m, 2)))
        older, old = None, None
        for d in range(m, LMAX + 1):
            if d == m:
                now = start
            elif d == m + 1:
                now = uz * ((2 * m + 1) * start * norm(d, m) / norm(m, m))
            else:
                ca = (2 * d - 1) / (d - m) * norm(d, m) / norm(d - 1, m)
                cb = (d + m - 1) / (d - m) * norm(d, m) / norm(d - 2, m)
                now = (ca * uz) * old - cb * older
            if m == 0:
                out[d * d + d] = now if d else jnp.full(ux.shape, start, F32)
            else:
                out[d * d + d + m] = cosine[m] * now
                out[d * d + d - m] = sine[m] * now
            older, old = old, now
    return out


def decode(i):
    def ring(q):
        return q + (q // 2) * (5 - 2 * q)

    return ring(i // 32), ring(i // 8 % 4), ring(i // 2 % 4), i % 2


def peer_of(i, sign, y, z, x, c):
    dy, dz, dx, dc = decode(i)
    return (
        lax.rem(y + sign * dy + 4, 4),
        lax.rem(z + sign * dz + 4, 4) * 8
        + lax.rem(x + sign * dx + 4, 4) * 2
        + lax.rem(c + dc, 2),
    )


def fused_kernel(
    labels,
    count,
    load,
    owner,
    atoms,
    coords,
    charge,
    shell,
    ghigh,
    glow,
    moments,
    potential,
    place,
    src,
    pay,
    arrived,
    ys,
    ws,
    hots,
    parts,
    acc,
    tables,
    reply,
    back,
    send_sem,
    recv_sem,
    reply_send,
    reply_recv,
):
    batches, slots = labels.shape
    spaces = batches * slots
    devices = pay.shape[0]
    owned = moments.shape[0]
    gy = lax.axis_index("gy")
    here_at = (lax.axis_index("gx"), gy // 8, lax.rem(gy, 8) // 2, lax.rem(gy, 2))

    barrier = pltpu.get_barrier_semaphore()

    @pl.loop(1, devices)
    def _(i):
        pl.semaphore_signal(
            barrier, inc=1, device_id=peer_of(i, 1, *here_at), device_id_type=MESH
        )

    for b in range(batches):

        @pl.loop(0, slots, unroll=4)
        def _(s):
            label = labels[b, s]
            target = owner[label]
            row = b * slots + s
            for c in range(3):
                place[c, pl.ds(row, 1), :] = jnp.full((1, 128), atoms[c, label], F32)
            place[3, pl.ds(row, 1), :] = jnp.full(
                (1, 128), (target // owned).astype(F32), F32
            )
            src[10, pl.ds(row, 1), :] = jnp.full(
                (1, 128), lax.rem(target, owned).astype(F32), F32
            )

    slot_rank = lax.broadcasted_iota(jnp.int32, (slots, 128), 0)
    lane = lax.broadcasted_iota(jnp.int32, (slots, 128), 1)
    lives = []
    for b in range(batches):
        live = jnp.clip(load[0] - b, 0, 1).astype(F32)
        slot_live = jnp.clip(count[b] - slot_rank, 0, 1).astype(F32)
        here = slice(b * slots, (b + 1) * slots)
        lives.append(jnp.where(lane == b, slot_live * live, 0.0))
        for h in range(2):
            points = slice(h * 128, (h + 1) * 128)
            squared = 0.0
            for c in range(3):
                offset = coords[c, b : b + 1, points] - place[c, here, :]
                src[2 * c + h, here, :] = offset
                squared = squared + offset * offset
            closeness = slot_live / (1.0 + squared)
            total = jnp.sum(closeness, axis=0, keepdims=True)
            scaled = charge[b : b + 1, points] * live / total
            src[6 + h, here, :] = shell[b, :, points].astype(F32)
            src[8 + h, here, :] = slot_live * scaled

    py, pg = peer_of(
        lax.broadcasted_iota(jnp.int32, (spaces, devices), 1), 1, *here_at
    )
    goes = (place[3] == (py * 32 + pg).astype(F32)).astype(F32)
    goes = goes.T.astype(BF16)
    flat_pay = pay.reshape(devices * PITCH, 128)
    for r in range(ROWS):
        high, rest = split(src[r])
        moved = dot(goes, high.astype(BF16))
        if r not in (6, 7, 10):
            middle, low = split(rest)
            moved = (
                moved + dot(goes, middle.astype(BF16)) + dot(goes, low.astype(BF16))
            )
        flat_pay[pl.ds(r, devices, stride=PITCH), :] = moved
    mine = dot(goes, jnp.concatenate(lives, axis=0).astype(BF16))
    mine = mine.T[:8].astype(BF16)

    pl.semaphore_wait(barrier, devices - 1)

    def piece(ref, i, size=1):
        return ref.at[pl.ds(i, size), pl.ds(0, ROWS)]

    for g in range(GROUPS):

        @pl.loop(max(g * WAVE, 1), (g + 1) * WAVE)
        def _(i):
            pltpu.make_async_remote_copy(
                src_ref=piece(pay, i),
                dst_ref=piece(arrived, i),
                send_sem=send_sem,
                recv_sem=recv_sem.at[g],
                device_id=peer_of(i, 1, *here_at),
                device_id_type=MESH,
            ).start()

    arrived[0] = pay[0]
    flat = arrived.reshape(devices * PITCH, 128)
    shell_rank = lax.broadcasted_iota(jnp.int32, (SHELLS, 128), 0).astype(F32)

    def shapes(g):
        for h in range(2):

            def row(r):
                return flat[pl.ds(g * 8 * PITCH + 2 * r + h, 8, stride=PITCH), :]

            dx, dy, dz = row(0), row(1), row(2)
            squared = dx * dx + dy * dy + dz * dz
            scale = lax.rsqrt(squared + SOFTEN)
            ws[h, pl.ds(pl.multiple_of(g * 8, 8), 8), :] = row(4) / (1.0 + squared)
            values = harmonics(dx * scale, dy * scale, dz * scale)
            for k in range(KP):
                value = values[k] if k < LM else jnp.zeros_like(dx)
                ys[h, pl.ds(g * 8 * KP + k, 8, stride=KP), :] = value

    def forward(i):
        stack, hot = [], []
        for h in range(2):
            y = ys[h, pl.ds(pl.multiple_of(i * KP, 8), KP), :]
            weighted = y * ws[h, pl.ds(i, 1), :]
            high, low = split(weighted)
            stack.append(jnp.concatenate([high, low], axis=0).astype(BF16))
            shells = flat[pl.ds(i * PITCH + 6 + h, 1), :]
            hot.append((shells == shell_rank).astype(F32).astype(BF16))
        hot = jnp.concatenate(hot, axis=1)
        hots[i] = hot
        both = dot(jnp.concatenate(stack, axis=1), hot, ((1,), (1,)))
        parts[pl.ds(i, KP, stride=SLOTP), :SHELLS] = both[:KP] + both[KP:]

    for g in range(GROUPS):
        first = max(g * WAVE, 1)
        size = (g + 1) * WAVE - first
        pltpu.make_async_remote_copy(
            src_ref=piece(pay, first, size),
            dst_ref=piece(arrived, first, size),
            send_sem=send_sem,
            recv_sem=recv_sem.at[g],
            device_id=(0, 0),
            device_id_type=MESH,
        ).wait_recv()

        @pl.loop(0, WAVE // 8)
        def _(q):
            shapes(g * (WAVE // 8) + q)

        @pl.loop(0, WAVE // 4)
        def _(q):
            for e in range(4):
                forward(g * WAVE + q * 4 + e)

    marks = flat[pl.ds(10, devices, stride=PITCH), :]
    picks = (
        marks == lax.broadcasted_iota(jnp.int32, (devices, 128), 1).astype(F32)
    ).astype(F32)
    gather = picks[:, :owned].astype(BF16)
    combine = picks.T[:owned].astype(BF16)
    combine = jnp.concatenate([combine, combine], axis=1)
    for k in range(LM):
        high, low = split(parts[pl.ds(k * SLOTP, devices), :SHELLS])
        both = jnp.concatenate([high, low], axis=0).astype(BF16)
        acc[k * owned : (k + 1) * owned, :SHELLS] = dot(combine, both)

    for d in range(LMAX + 1):
        begin, end = d * d, (d + 1) * (d + 1)
        high, low = split(acc[begin * owned : end * owned, :SHELLS])
        high, low = high.astype(BF16), low.astype(BF16)
        table = dot(high, ghigh[d]) + dot(low, ghigh[d]) + dot(high, glow[d])
        thigh, tlow = split(table)
        lane_rank = lax.broadcasted_iota(jnp.int32, table.shape, 1)
        table = jnp.where(lane_rank < SHELLS, thigh, tlow).astype(BF16)
        for k in range(begin, end):
            tables[k * SLOTP : k * SLOTP + devices, :] = dot(
                gather, table[(k - begin) * owned : (k - begin + 1) * owned]
            )
    for k in range(LM, KP):
        tables[k * SLOTP : k * SLOTP + devices, :] = jnp.zeros((devices, 128), F32)

    def evaluate(i):
        table = tables[pl.ds(i, KP, stride=SLOTP), :].astype(BF16)
        hot = hots[i]
        picked = dot(table, jnp.concatenate([hot, hot], axis=0))
        for h in range(2):
            y = ys[h, pl.ds(pl.multiple_of(i * KP, 8), KP), :]
            total = jnp.sum(
                picked[:, h * 128 : (h + 1) * 128] * y, axis=0, keepdims=True
            )
            reply[pl.ds(i, 1), h, :] = total

    def answer(g):
        @pl.loop(max(g * WAVE, 1), (g + 1) * WAVE)
        def _(i):
            pltpu.make_async_remote_copy(
                src_ref=reply.at[pl.ds(i, 1)],
                dst_ref=back.at[pl.ds(i, 1)],
                send_sem=reply_send,
                recv_sem=reply_recv,
                device_id=peer_of(i, -1, *here_at),
                device_id_type=MESH,
            ).start()

    for g in reversed(range(GROUPS)):

        @pl.loop(0, WAVE // 4)
        def _(q):
            for e in range(4):
                evaluate(g * WAVE + q * 4 + e)

        if g + 1 < GROUPS:
            answer(g + 1)
    for k in range(0, LM, 2):
        first = acc[k * owned : (k + 1) * owned, :SHELLS]
        if k + 1 < LM:
            second = acc[(k + 1) * owned : (k + 2) * owned, :SHELLS]
            first = jnp.concatenate([first, second], axis=1)
        moments[:, k * SHELLS : min(k + 2, LM) * SHELLS] = first
    answer(0)
    back[0] = reply[0]

    everything = pltpu.make_async_remote_copy(
        src_ref=piece(pay, 1, devices - 1),
        dst_ref=piece(arrived, 1, devices - 1),
        send_sem=send_sem,
        recv_sem=recv_sem.at[0],
        device_id=(0, 0),
        device_id_type=MESH,
    )
    everything.wait_send()
    answers = pltpu.make_async_remote_copy(
        src_ref=reply.at[pl.ds(1, devices - 1)],
        dst_ref=back.at[pl.ds(1, devices - 1)],
        send_sem=reply_send,
        recv_sem=reply_recv,
        device_id=(0, 0),
        device_id_type=MESH,
    )
    answers.wait_send()
    answers.wait_recv()
    for h in range(2):
        high, rest = split(back[:, h, :])
        middle, low = split(rest)
        total = (
            dot(mine, high.astype(BF16))
            + dot(mine, middle.astype(BF16))
            + dot(mine, low.astype(BF16))
        )
        potential[:, h * 128 : (h + 1) * 128] = total[:batches]


VMEM = pl.BlockSpec(memory_space=pltpu.VMEM)
SMEM = pl.BlockSpec(memory_space=pltpu.SMEM)


def body(
    point_coords,
    charge,
    shell_index,
    neighbours,
    neighbour_count,
    batch_load,
    atom_coords,
    owner_slot,
):
    batches = charge.shape[0]
    slots = neighbours.shape[1]
    devices = lax.axis_size("gx") * lax.axis_size("gy")
    owned = owner_slot.shape[0] // devices
    spaces = batches * slots
    sds = jax.ShapeDtypeStruct
    ghigh, glow = green_pair()
    moments, potential = pl.pallas_call(
        fused_kernel,
        out_shape=(sds((owned, LM * SHELLS), F32), sds(charge.shape, F32)),
        in_specs=[SMEM] * 5 + [VMEM] * 5,
        out_specs=(VMEM, VMEM),
        scratch_shapes=[
            pltpu.VMEM((4, spaces, 128), F32),
            pltpu.VMEM((ROWS, spaces, 128), F32),
            pltpu.VMEM((devices, PITCH, 128), F32),
            pltpu.VMEM((devices, PITCH, 128), F32),
            pltpu.VMEM((2, devices * KP, 128), F32),
            pltpu.VMEM((2, devices, 128), F32),
            pltpu.VMEM((devices, SHELLS, 256), BF16),
            pltpu.VMEM((KP * SLOTP, 128), F32),
            pltpu.VMEM((LM * owned, 128), F32),
            pltpu.VMEM((KP * SLOTP, 128), F32),
            pltpu.VMEM((devices, 2, 128), F32),
            pltpu.VMEM((devices, 2, 128), F32),
            pltpu.SemaphoreType.DMA,
            pltpu.SemaphoreType.DMA((GROUPS,)),
            pltpu.SemaphoreType.DMA,
            pltpu.SemaphoreType.DMA,
        ],
        compiler_params=pltpu.CompilerParams(collective_id=0, has_side_effects=True),
        name="fused",
    )(
        neighbours,
        neighbour_count,
        batch_load,
        owner_slot,
        atom_coords,
        jnp.transpose(point_coords, (1, 0, 2)),
        charge,
        shell_index,
        jnp.asarray(ghigh),
        jnp.asarray(glow),
    )
    return (potential, moments)


def solution(mesh):
    return jax.shard_map(
        body,
        mesh=mesh,
        in_specs=(
            P(("gx", "gy"), None, None),
            P(("gx", "gy"), None),
            P(("gx", "gy"), None, None),
            P(("gx", "gy"), None),
            P(("gx", "gy")),
            P(("gx", "gy")),
            P(),
            P(),
        ),
        out_specs=(P(("gx", "gy"), None), P(("gx", "gy"), None)),
        check_vma=False,
    )
```

time: 67.7 us -> 59.4 us (0.88)
  Pallas kernels: 63.5 us -> 54.8 us
    pallas_call x4 -> x1, Pallas kernels: 63.5 us -> 54.8 us  [body(): pl.pallas_call(fused_kernel, out_shape=(sds((owned, LM * SHELLS), F32), s...]
where the time goes in v2:
time: 59.4 us; the launch traced here: 59.2 us
  Pallas kernels  54.8 us (92%)
  local copies, waits for them, and re-layouts  3.05 us (5%)
  between operations  1.29 us (2%)
    pallas_call x1, Pallas kernels, body(): pl.pallas_call(fused_kernel, out_shape=(sds((owned, LM * SHELLS), F32), s...  54.8 us
    unnamed x2, local copies, waits for them, and re-layouts  3.05 us

profile of v2, /device:TPU:1, one launch (start us, length us, event | category | flops | bytes accessed | tf_op | source)
XLA Modules:
  0.0 59.2 jit_solution(11146390456190852318)
XLA Ops:
  1.3 54.8 %fused.1 = (f32[32,3136]{1,0:T(8,128)}, f32[4,256]{1,0:T(4,128)}) custom-call(s32[4,32]{1,0:T(4,128)} %labels.1, s32[4]{0:T(128)} %count.1, s32[1]{0:T(128)S(6)} %copy.14.load, s32[4096]{0:T(1024)} %owner.1, f32[3,4096]{1,0:T(4,128)} %atoms.1, f32[3,4,256]{2,1,0:T(4,128)} %bitcast.1, f32[4,256]{1,0:T(4,128)} %charge.1, s32[4,32,256]{2,1,0:T(8,128)} %shell.1, ...), custom_call_target="tpu_custom_call" | custom-call | tf_op jit(solution)/shard_map/fused/pallas_call | solution.py:400
  56.1 1.3 %copy.15 = f32[4,256]{1,0:T(4,128)} copy(f32[4,256]{1,0:T(4,128)} %get-tuple-element.8) | data formatting | bytes 8192
  57.4 1.8 %copy.16 = f32[32,3136]{1,0:T(8,128)} copy(f32[32,3136]{1,0:T(8,128)} %get-tuple-element.9) | data formatting | bytes 802816

commit v3 on v2

--- a/solution.py
+++ b/solution.py
@@ -19,8 +19,7 @@
 ROWS = 11
 PITCH = 16
 SLOTP = 136
-GROUPS = 8
-WAVE = 16
+WAVE = 32
 
 
 def green_pair():
@@ -89,21 +88,22 @@
     return out
 
 
-def decode(i):
-    def ring(q):
-        return q + (q // 2) * (5 - 2 * q)
-
-    return ring(i // 32), ring(i // 8 % 4), ring(i // 2 % 4), i % 2
-
-
-def peer_of(i, sign, y, z, x, c):
-    dy, dz, dx, dc = decode(i)
-    return (
-        lax.rem(y + sign * dy + 4, 4),
-        lax.rem(z + sign * dz + 4, 4) * 8
-        + lax.rem(x + sign * dx + 4, 4) * 2
-        + lax.rem(c + dc, 2),
-    )
+def visiting_order():
+    every = [
+        (dy, dz, dx, dc)
+        for dy in range(4)
+        for dz in range(4)
+        for dx in range(4)
+        for dc in range(2)
+    ]
+
+    def far(t):
+        return sum(min(v, 4 - v) for v in t[:3])
+
+    return every[:1] + sorted(every[1:], key=far, reverse=True)
+
+
+ORDER = visiting_order()
 
 
 def fused_kernel(
@@ -117,8 +117,10 @@
     shell,
     ghigh,
     glow,
+    steps,
     moments,
-    potential,
+    mine,
+    back,
     place,
     src,
     pay,
@@ -130,7 +132,6 @@
     acc,
     tables,
     reply,
-    back,
     send_sem,
     recv_sem,
     reply_send,
@@ -141,14 +142,24 @@
     devices = pay.shape[0]
     owned = moments.shape[0]
     gy = lax.axis_index("gy")
-    here_at = (lax.axis_index("gx"), gy // 8, lax.rem(gy, 8) // 2, lax.rem(gy, 2))
+    at = (lax.axis_index("gx"), gy // 8, lax.rem(gy, 8) // 2, lax.rem(gy, 2))
+    spans = (4, 4, 4, 2)
+    moved_to = [
+        [lax.rem(at[axis] + step, spans[axis]) for step in range(spans[axis])]
+        for axis in range(4)
+    ]
+
+    def peer(i, sign):
+        y, z, x, c = [
+            moved_to[axis][sign * step % spans[axis]]
+            for axis, step in enumerate(ORDER[i])
+        ]
+        return (y, z * 8 + x * 2 + c)
 
     barrier = pltpu.get_barrier_semaphore()
-
-    @pl.loop(1, devices)
-    def _(i):
+    for i in range(1, devices):
         pl.semaphore_signal(
-            barrier, inc=1, device_id=peer_of(i, 1, *here_at), device_id_type=MESH
+            barrier, inc=1, device_id=peer(i, -1), device_id_type=MESH
         )
 
     for b in range(batches):
@@ -188,10 +199,11 @@
             src[6 + h, here, :] = shell[b, :, points].astype(F32)
             src[8 + h, here, :] = slot_live * scaled
 
-    py, pg = peer_of(
-        lax.broadcasted_iota(jnp.int32, (spaces, devices), 1), 1, *here_at
-    )
-    goes = (place[3] == (py * 32 + pg).astype(F32)).astype(F32)
+    row_of = 0
+    for axis in range(4):
+        there = lax.rem(steps[axis : axis + 1, :] + at[axis], spans[axis])
+        row_of = row_of * spans[axis] + there
+    goes = (place[3] == row_of.astype(F32)).astype(F32)
     goes = goes.T.astype(BF16)
     flat_pay = pay.reshape(devices * PITCH, 128)
     for r in range(ROWS):
@@ -203,26 +215,23 @@
                 moved + dot(goes, middle.astype(BF16)) + dot(goes, low.astype(BF16))
             )
         flat_pay[pl.ds(r, devices, stride=PITCH), :] = moved
-    mine = dot(goes, jnp.concatenate(lives, axis=0).astype(BF16))
-    mine = mine.T[:8].astype(BF16)
+    lives = dot(goes, jnp.concatenate(lives, axis=0).astype(BF16))
+    mine[...] = lives.T[:8]
 
     pl.semaphore_wait(barrier, devices - 1)
 
     def piece(ref, i, size=1):
         return ref.at[pl.ds(i, size), pl.ds(0, ROWS)]
 
-    for g in range(GROUPS):
-
-        @pl.loop(max(g * WAVE, 1), (g + 1) * WAVE)
-        def _(i):
-            pltpu.make_async_remote_copy(
-                src_ref=piece(pay, i),
-                dst_ref=piece(arrived, i),
-                send_sem=send_sem,
-                recv_sem=recv_sem.at[g],
-                device_id=peer_of(i, 1, *here_at),
-                device_id_type=MESH,
-            ).start()
+    for i in range(1, devices):
+        pltpu.make_async_remote_copy(
+            src_ref=piece(pay, i),
+            dst_ref=piece(arrived, i),
+            send_sem=send_sem,
+            recv_sem=recv_sem.at[i // WAVE],
+            device_id=peer(i, 1),
+            device_id_type=MESH,
+        ).start()
 
     arrived[0] = pay[0]
     flat = arrived.reshape(devices * PITCH, 128)
@@ -257,26 +266,32 @@
         both = dot(jnp.concatenate(stack, axis=1), hot, ((1,), (1,)))
         parts[pl.ds(i, KP, stride=SLOTP), :SHELLS] = both[:KP] + both[KP:]
 
-    for g in range(GROUPS):
-        first = max(g * WAVE, 1)
-        size = (g + 1) * WAVE - first
+    def landed(g, size):
         pltpu.make_async_remote_copy(
-            src_ref=piece(pay, first, size),
-            dst_ref=piece(arrived, first, size),
+            src_ref=piece(pay, 1, size),
+            dst_ref=piece(arrived, 1, size),
             send_sem=send_sem,
             recv_sem=recv_sem.at[g],
             device_id=(0, 0),
             device_id_type=MESH,
         ).wait_recv()
 
+    @pl.loop(0, devices // WAVE)
+    def _(g):
+        @pl.when(g == 0)
+        def _():
+            landed(g, WAVE - 1)
+
+        @pl.when(g > 0)
+        def _():
+            landed(g, WAVE)
+
         @pl.loop(0, WAVE // 8)
         def _(q):
             shapes(g * (WAVE // 8) + q)
 
-        @pl.loop(0, WAVE // 4)
-        def _(q):
-            for e in range(4):
-                forward(g * WAVE + q * 4 + e)
+        for e in range(WAVE):
+            forward(g * WAVE + e)
 
     marks = flat[pl.ds(10, devices, stride=PITCH), :]
     picks = (
@@ -314,37 +329,32 @@
             total = jnp.sum(
                 picked[:, h * 128 : (h + 1) * 128] * y, axis=0, keepdims=True
             )
-            reply[pl.ds(i, 1), h, :] = total
+            reply[i, h : h + 1, :] = total
 
     def answer(g):
-        @pl.loop(max(g * WAVE, 1), (g + 1) * WAVE)
-        def _(i):
+        for i in range(max(g * WAVE, 1), (g + 1) * WAVE):
             pltpu.make_async_remote_copy(
-                src_ref=reply.at[pl.ds(i, 1)],
-                dst_ref=back.at[pl.ds(i, 1)],
+                src_ref=reply.at[i],
+                dst_ref=back.at[i],
                 send_sem=reply_send,
                 recv_sem=reply_recv,
-                device_id=peer_of(i, -1, *here_at),
+                device_id=peer(i, -1),
                 device_id_type=MESH,
             ).start()
 
-    for g in reversed(range(GROUPS)):
-
-        @pl.loop(0, WAVE // 4)
-        def _(q):
-            for e in range(4):
-                evaluate(g * WAVE + q * 4 + e)
-
-        if g + 1 < GROUPS:
-            answer(g + 1)
+    for g in range(devices // WAVE):
+        for e in range(WAVE):
+            evaluate(g * WAVE + e)
+        if g:
+            answer(g - 1)
+    back[0] = reply[0]
+    answer(devices // WAVE - 1)
     for k in range(0, LM, 2):
         first = acc[k * owned : (k + 1) * owned, :SHELLS]
         if k + 1 < LM:
             second = acc[(k + 1) * owned : (k + 2) * owned, :SHELLS]
             first = jnp.concatenate([first, second], axis=1)
         moments[:, k * SHELLS : min(k + 2, LM) * SHELLS] = first
-    answer(0)
-    back[0] = reply[0]
 
     everything = pltpu.make_async_remote_copy(
         src_ref=piece(pay, 1, devices - 1),
@@ -365,15 +375,21 @@
     )
     answers.wait_send()
     answers.wait_recv()
+
+
+def finish_kernel(mine, back, sums, potential, moments):
+    batches = potential.shape[0]
+    chosen = mine[...].astype(BF16)
     for h in range(2):
         high, rest = split(back[:, h, :])
         middle, low = split(rest)
         total = (
-            dot(mine, high.astype(BF16))
-            + dot(mine, middle.astype(BF16))
-            + dot(mine, low.astype(BF16))
+            dot(chosen, high.astype(BF16))
+            + dot(chosen, middle.astype(BF16))
+            + dot(chosen, low.astype(BF16))
         )
         potential[:, h * 128 : (h + 1) * 128] = total[:batches]
+    moments[...] = sums[...]
 
 
 VMEM = pl.BlockSpec(memory_space=pltpu.VMEM)
@@ -397,11 +413,15 @@
     spaces = batches * slots
     sds = jax.ShapeDtypeStruct
     ghigh, glow = green_pair()
-    moments, potential = pl.pallas_call(
+    sums, mine, back = pl.pallas_call(
         fused_kernel,
-        out_shape=(sds((owned, LM * SHELLS), F32), sds(charge.shape, F32)),
-        in_specs=[SMEM] * 5 + [VMEM] * 5,
-        out_specs=(VMEM, VMEM),
+        out_shape=(
+            sds((owned, LM * SHELLS), F32),
+            sds((8, devices), F32),
+            sds((devices, 2, 128), F32),
+        ),
+        in_specs=[SMEM] * 5 + [VMEM] * 6,
+        out_specs=(VMEM, VMEM, VMEM),
         scratch_shapes=[
             pltpu.VMEM((4, spaces, 128), F32),
             pltpu.VMEM((ROWS, spaces, 128), F32),
@@ -414,9 +434,8 @@
             pltpu.VMEM((LM * owned, 128), F32),
             pltpu.VMEM((KP * SLOTP, 128), F32),
             pltpu.VMEM((devices, 2, 128), F32),
-            pltpu.VMEM((devices, 2, 128), F32),
             pltpu.SemaphoreType.DMA,
-            pltpu.SemaphoreType.DMA((GROUPS,)),
+            pltpu.SemaphoreType.DMA((devices // WAVE,)),
             pltpu.SemaphoreType.DMA,
             pltpu.SemaphoreType.DMA,
         ],
@@ -433,7 +452,15 @@
         shell_index,
         jnp.asarray(ghigh),
         jnp.asarray(glow),
+        jnp.asarray(np.array(ORDER, dtype=np.int32).T),
     )
+    potential, moments = pl.pallas_call(
+        finish_kernel,
+        out_shape=(sds(charge.shape, F32), sds(sums.shape, F32)),
+        in_specs=[VMEM] * 3,
+        out_specs=(VMEM, VMEM),
+        name="finish",
+    )(mine, back, sums)
     return (potential, moments)
 
 

time: 59.4 us -> 40.6 us (0.68)
  Pallas kernels: 54.8 us -> 39.1 us
  local copies, waits for them, and re-layouts: 3.05 us -> 0 us
    pallas_call x1, Pallas kernels: 54.8 us -> 36.7 us  [body(): pl.pallas_call(fused_kernel, out_shape=(sds((owned, LM * SHELLS), F32), s...]
    unnamed x2 -> x0, local copies, waits for them, and re-layouts: 3.05 us -> none
    pallas_call x0 -> x1, Pallas kernels: none -> 2.39 us  [body(): pl.pallas_call(finish_kernel, out_shape=(sds(charge.shape, F32), sds(sums...]
where the time goes in v3:
time: 40.6 us; the launch traced here: 40.4 us
  Pallas kernels  39.1 us (96%)
  between operations  1.29 us (3%)
    pallas_call x1, Pallas kernels, body(): pl.pallas_call(fused_kernel, out_shape=(sds((owned, LM * SHELLS), F32), s...  36.7 us
    pallas_call x1, Pallas kernels, body(): pl.pallas_call(finish_kernel, out_shape=(sds(charge.shape, F32), sds(sums...  2.39 us

profile of v3, /device:TPU:1, one launch (start us, length us, event | category | flops | bytes accessed | tf_op | source)
XLA Modules:
  0.0 40.4 jit_solution(11398710005492533997)
XLA Ops:
  1.3 36.7 %fused.1 = (f32[32,3136]{1,0:T(8,128)}, f32[8,128]{1,0:T(8,128)}, f32[128,2,128]{2,1,0:T(2,128)}) custom-call(s32[4,32]{1,0:T(4,128)} %labels.1, s32[4]{0:T(128)} %count.1, s32[1]{0:T(128)S(6)} %copy.13.load, s32[4096]{0:T(1024)} %owner.1, f32[3,4096]{1,0:T(4,128)} %atoms.1, f32[3,4,256]{2,1,0:T(4,128)} %bitcast.1, f32[4,256]{1,0:T(4,128)} %charge.1, ...), custom_call_target="tpu_custom_call" | custom-call | tf_op jit(solution)/shard_map/fused/pallas_call | solution.py:416
  38.0 2.4 %finish.1 = (f32[4,256]{1,0:T(4,128)}, f32[32,3136]{1,0:T(8,128)}) custom-call(f32[8,128]{1,0:T(8,128)} %get-tuple-element.5.mine, f32[128,2,128]{2,1,0:T(2,128)} %get-tuple-element.6.back, f32[32,3136]{1,0:T(8,128)} %get-tuple-element.7.sums), custom_call_target="tpu_custom_call" | custom-call | tf_op jit(solution)/shard_map/finish/pallas_call | solution.py:457

commit v4 on v3

--- a/solution.py
+++ b/solution.py
@@ -107,40 +107,40 @@
 
 
 def fused_kernel(
-    labels,
-    count,
-    load,
-    owner,
-    atoms,
-    coords,
-    charge,
-    shell,
-    ghigh,
-    glow,
-    steps,
-    moments,
-    mine,
-    back,
-    place,
-    src,
-    pay,
-    arrived,
-    ys,
-    ws,
-    hots,
-    parts,
-    acc,
-    tables,
-    reply,
-    send_sem,
-    recv_sem,
-    reply_send,
-    reply_recv,
+    *refs,
 ):
+    load, given, refs = refs[0], refs[1:11], refs[11:]
+    sums, mine, back = refs[:3]
+    held, refs = refs[3:13], refs[13:]
+    (
+        place,
+        src,
+        pay,
+        arrived,
+        ys,
+        ws,
+        hots,
+        parts,
+        acc,
+        tables,
+        reply,
+        load_sem,
+        send_sem,
+        recv_sem,
+        reply_send,
+        reply_recv,
+    ) = refs
+    labels, count, owner, atoms, coords, charge, shell, ghigh, glow, steps = held
+    loads = [
+        pltpu.make_async_copy(given[n], held[n], load_sem.at[n])
+        for n in range(len(held))
+    ]
+    for one in loads:
+        one.start()
     batches, slots = labels.shape
     spaces = batches * slots
     devices = pay.shape[0]
-    owned = moments.shape[0]
+    owned = sums.shape[0]
     gy = lax.axis_index("gy")
     at = (lax.axis_index("gx"), gy // 8, lax.rem(gy, 8) // 2, lax.rem(gy, 2))
     spans = (4, 4, 4, 2)
@@ -162,6 +162,8 @@
             barrier, inc=1, device_id=peer(i, -1), device_id_type=MESH
         )
 
+    for one in loads:
+        one.wait()
     for b in range(batches):
 
         @pl.loop(0, slots, unroll=4)
@@ -313,10 +315,15 @@
         thigh, tlow = split(table)
         lane_rank = lax.broadcasted_iota(jnp.int32, table.shape, 1)
         table = jnp.where(lane_rank < SHELLS, thigh, tlow).astype(BF16)
-        for k in range(begin, end):
-            tables[k * SLOTP : k * SLOTP + devices, :] = dot(
-                gather, table[(k - begin) * owned : (k - begin + 1) * owned]
-            )
+        for k in range(begin, end, 2):
+            rows = [
+                table[(n - begin) * owned : (n - begin + 1) * owned]
+                for n in range(k, min(k + 2, end))
+            ]
+            picked = dot(gather, jnp.concatenate(rows, axis=1))
+            for n in range(len(rows)):
+                at_k = (k + n) * SLOTP
+                tables[at_k : at_k + devices, :] = picked[:, n * 128 : (n + 1) * 128]
     for k in range(LM, KP):
         tables[k * SLOTP : k * SLOTP + devices, :] = jnp.zeros((devices, 128), F32)
 
@@ -331,8 +338,8 @@
             )
             reply[i, h : h + 1, :] = total
 
-    def answer(g):
-        for i in range(max(g * WAVE, 1), (g + 1) * WAVE):
+    def answer(begin, end):
+        for i in range(max(begin, 1), end):
             pltpu.make_async_remote_copy(
                 src_ref=reply.at[i],
                 dst_ref=back.at[i],
@@ -342,19 +349,20 @@
                 device_id_type=MESH,
             ).start()
 
-    for g in range(devices // WAVE):
-        for e in range(WAVE):
-            evaluate(g * WAVE + e)
-        if g:
-            answer(g - 1)
+    cuts = (0, 16, 32, 64, 96, devices)
+    for n in range(len(cuts) - 1):
+        for i in range(cuts[n], cuts[n + 1]):
+            evaluate(i)
+        if n:
+            answer(cuts[n - 1], cuts[n])
     back[0] = reply[0]
-    answer(devices // WAVE - 1)
+    answer(cuts[-2], cuts[-1])
     for k in range(0, LM, 2):
         first = acc[k * owned : (k + 1) * owned, :SHELLS]
         if k + 1 < LM:
             second = acc[(k + 1) * owned : (k + 2) * owned, :SHELLS]
             first = jnp.concatenate([first, second], axis=1)
-        moments[:, k * SHELLS : min(k + 2, LM) * SHELLS] = first
+        sums[:, k * SHELLS : min(k + 2, LM) * SHELLS] = first
 
     everything = pltpu.make_async_remote_copy(
         src_ref=piece(pay, 1, devices - 1),
@@ -393,6 +401,7 @@
 
 
 VMEM = pl.BlockSpec(memory_space=pltpu.VMEM)
+HBM = pl.BlockSpec(memory_space=pltpu.HBM)
 SMEM = pl.BlockSpec(memory_space=pltpu.SMEM)
 
 
@@ -406,7 +415,7 @@
     atom_coords,
     owner_slot,
 ):
-    batches = charge.shape[0]
+    batches, points = charge.shape
     slots = neighbours.shape[1]
     devices = lax.axis_size("gx") * lax.axis_size("gy")
     owned = owner_slot.shape[0] // devices
@@ -420,9 +429,19 @@
             sds((8, devices), F32),
             sds((devices, 2, 128), F32),
         ),
-        in_specs=[SMEM] * 5 + [VMEM] * 6,
+        in_specs=[SMEM] + [HBM] * 10,
         out_specs=(VMEM, VMEM, VMEM),
         scratch_shapes=[
+            pltpu.SMEM((batches, slots), jnp.int32),
+            pltpu.SMEM((batches,), jnp.int32),
+            pltpu.SMEM(owner_slot.shape, jnp.int32),
+            pltpu.SMEM(atom_coords.shape, F32),
+            pltpu.VMEM((3, batches, points), F32),
+            pltpu.VMEM((batches, points), F32),
+            pltpu.VMEM((batches, slots, points), jnp.int32),
+            pltpu.VMEM(ghigh.shape, BF16),
+            pltpu.VMEM(glow.shape, BF16),
+            pltpu.VMEM((4, devices), jnp.int32),
             pltpu.VMEM((4, spaces, 128), F32),
             pltpu.VMEM((ROWS, spaces, 128), F32),
             pltpu.VMEM((devices, PITCH, 128), F32),
@@ -434,31 +453,40 @@
             pltpu.VMEM((LM * owned, 128), F32),
             pltpu.VMEM((KP * SLOTP, 128), F32),
             pltpu.VMEM((devices, 2, 128), F32),
+            pltpu.SemaphoreType.DMA((10,)),
             pltpu.SemaphoreType.DMA,
             pltpu.SemaphoreType.DMA((devices // WAVE,)),
             pltpu.SemaphoreType.DMA,
             pltpu.SemaphoreType.DMA,
         ],
-        compiler_params=pltpu.CompilerParams(collective_id=0, has_side_effects=True),
+        compiler_params=pltpu.CompilerParams(
+            collective_id=0, has_side_effects=True, vmem_limit_bytes=34 << 20
+        ),
         name="fused",
     )(
-        neighbours,
-        neighbour_count,
         batch_load,
-        owner_slot,
-        atom_coords,
-        jnp.transpose(point_coords, (1, 0, 2)),
-        charge,
-        shell_index,
-        jnp.asarray(ghigh),
-        jnp.asarray(glow),
-        jnp.asarray(np.array(ORDER, dtype=np.int32).T),
+        *[
+            pltpu.with_memory_space_constraint(one, pltpu.HBM)
+            for one in (
+                neighbours,
+                neighbour_count,
+                owner_slot,
+                atom_coords,
+                jnp.transpose(point_coords, (1, 0, 2)),
+                charge,
+                shell_index,
+                jnp.asarray(ghigh),
+                jnp.asarray(glow),
+                jnp.asarray(np.array(ORDER, dtype=np.int32).T),
+            )
+        ]
     )
     potential, moments = pl.pallas_call(
         finish_kernel,
         out_shape=(sds(charge.shape, F32), sds(sums.shape, F32)),
         in_specs=[VMEM] * 3,
         out_specs=(VMEM, VMEM),
+        compiler_params=pltpu.CompilerParams(vmem_limit_bytes=4 << 20),
         name="finish",
     )(mine, back, sums)
     return (potential, moments)

time: 40.6 us -> 36.7 us (0.904)
  Pallas kernels: 39.1 us -> 35.3 us
    pallas_call x1, Pallas kernels: 36.7 us -> 33.9 us  [body(): pl.pallas_call(fused_kernel, out_shape=(sds((owned, LM * SHELLS), F32), s...]
    pallas_call x1, Pallas kernels: 2.39 us -> 1.31 us  [body(): pl.pallas_call(finish_kernel, out_shape=(sds(charge.shape, F32), sds(sums...]
where the time goes in v4:
time: 36.7 us; the launch traced here: 36.5 us
  Pallas kernels  35.3 us (96%)
  between operations  1.29 us (4%)
    pallas_call x1, Pallas kernels, body(): pl.pallas_call(fused_kernel, out_shape=(sds((owned, LM * SHELLS), F32), s...  33.9 us
    pallas_call x1, Pallas kernels, body(): pl.pallas_call(finish_kernel, out_shape=(sds(charge.shape, F32), sds(sums...  1.31 us

profile of v4, /device:TPU:1, one launch (start us, length us, event | category | flops | bytes accessed | tf_op | source)
XLA Modules:
  0.0 36.5 jit_solution(1940240673178161955)
XLA Ops:
  1.3 33.9 %fused.1 = (f32[32,3136]{1,0:T(8,128)S(1)}, f32[8,128]{1,0:T(8,128)S(1)}, f32[128,2,128]{2,1,0:T(2,128)S(1)}) custom-call(s32[1]{0:T(128)S(6)} %copy.13.refs_0_, s32[4,32]{1,0:T(4,128)} %refs_1_.1, s32[4]{0:T(128)} %refs_2_.1, s32[4096]{0:T(1024)} %refs_3_.1, f32[3,4096]{1,0:T(4,128)} %refs_4_.1, f32[3,4,256]{2,1,0:T(4,128)} %bitcast.1, f32[4,256]{1,0:T(4,128)} %refs_6_.1, ...), custom_call_target="tpu_custom_call" | custom-call | tf_op jit(solution)/shard_map/fused/pallas_call | solution.py:425
  35.2 1.3 %finish.1 = (f32[4,256]{1,0:T(4,128)}, f32[32,3136]{1,0:T(8,128)}) custom-call(f32[8,128]{1,0:T(8,128)S(1)} %get-tuple-element.5.mine, f32[128,2,128]{2,1,0:T(2,128)S(1)} %get-tuple-element.6.back, f32[32,3136]{1,0:T(8,128)S(1)} %get-tuple-element.7.sums), custom_call_target="tpu_custom_call" | custom-call | tf_op jit(solution)/shard_map/finish/pallas_call | solution.py:484

commit v5 on v4

--- a/solution.py
+++ b/solution.py
@@ -15,6 +15,7 @@
 LMAX = 6
 LM = 49
 KP = 56
+HALF = 24
 SOFTEN = 0.01
 ROWS = 11
 PITCH = 16
@@ -22,7 +23,7 @@
 WAVE = 32
 
 
-def green_pair():
+def green_blocks():
     rank = np.arange(SHELLS, dtype=np.float64)
     radius = 0.5 * np.exp(2.3 * rank / SHELLS)
     nearer = np.minimum(radius[:, None], radius[None, :])
@@ -36,7 +37,9 @@
     full = np.concatenate([full, full], axis=2).astype(np.float32)
     high = full.astype(jnp.bfloat16)
     low = (full - high.astype(np.float32)).astype(jnp.bfloat16)
-    return high, low
+    upper = np.concatenate([high, low], axis=2)
+    lower = np.concatenate([high, np.zeros_like(low)], axis=2)
+    return np.concatenate([upper, lower], axis=1)
 
 
 def split(x):
@@ -109,9 +112,9 @@
 def fused_kernel(
     *refs,
 ):
-    load, given, refs = refs[0], refs[1:11], refs[11:]
+    load, given, refs = refs[0], refs[1:10], refs[10:]
     sums, mine, back = refs[:3]
-    held, refs = refs[3:13], refs[13:]
+    held, refs = refs[3:12], refs[12:]
     (
         place,
         src,
@@ -122,6 +125,7 @@
         hots,
         parts,
         acc,
+        small,
         tables,
         reply,
         load_sem,
@@ -130,7 +134,7 @@
         reply_send,
         reply_recv,
     ) = refs
-    labels, count, owner, atoms, coords, charge, shell, ghigh, glow, steps = held
+    labels, count, owner, atoms, coords, charge, shell, green, steps = held
     loads = [
         pltpu.make_async_copy(given[n], held[n], load_sem.at[n])
         for n in range(len(held))
@@ -161,6 +165,22 @@
         pl.semaphore_signal(
             barrier, inc=1, device_id=peer(i, -1), device_id_type=MESH
         )
+
+    top = jnp.where(
+        lax.broadcasted_iota(jnp.int32, (8, 128), 0) == 0,
+        math.sqrt(1 / (4 * math.pi)),
+        0.0,
+    ).astype(F32)
+
+    @pl.loop(0, devices)
+    def _(i):
+        for h in range(2):
+            ys[h, pl.ds(pl.multiple_of(i * KP, 8), 8), :] = top
+            ys[h, pl.ds(pl.multiple_of(i * KP + KP - 8, 8), 8), :] = jnp.zeros_like(top)
+
+    for k in range(LM, KP):
+        tables[k * SLOTP : k * SLOTP + devices, :] = jnp.zeros((devices, 128), F32)
+    parts[(HALF * SLOTP) :, :] = jnp.zeros((SLOTP, 128), F32)
 
     for one in loads:
         one.wait()
@@ -250,9 +270,8 @@
             scale = lax.rsqrt(squared + SOFTEN)
             ws[h, pl.ds(pl.multiple_of(g * 8, 8), 8), :] = row(4) / (1.0 + squared)
             values = harmonics(dx * scale, dy * scale, dz * scale)
-            for k in range(KP):
-                value = values[k] if k < LM else jnp.zeros_like(dx)
-                ys[h, pl.ds(g * 8 * KP + k, 8, stride=KP), :] = value
+            for k in range(1, LM):
+                ys[h, pl.ds(g * 8 * KP + k, 8, stride=KP), :] = values[k]
 
     def forward(i):
         stack, hot = [], []
@@ -266,7 +285,11 @@
         hot = jnp.concatenate(hot, axis=1)
         hots[i] = hot
         both = dot(jnp.concatenate(stack, axis=1), hot, ((1,), (1,)))
-        parts[pl.ds(i, KP, stride=SLOTP), :SHELLS] = both[:KP] + both[KP:]
+        part = both[:KP] + both[KP:]
+        parts[pl.ds(i, HALF, stride=SLOTP), :] = jnp.concatenate(
+            [part[:HALF], part[HALF : 2 * HALF]], axis=1
+        )
+        parts[pl.ds(HALF * SLOTP + i, 1), :SHELLS] = part[2 * HALF : LM]
 
     def landed(g, size):
         pltpu.make_async_remote_copy(
@@ -288,8 +311,7 @@
         def _():
             landed(g, WAVE)
 
-        @pl.loop(0, WAVE // 8)
-        def _(q):
+        for q in range(WAVE // 8):
             shapes(g * (WAVE // 8) + q)
 
         for e in range(WAVE):
@@ -302,30 +324,32 @@
     gather = picks[:, :owned].astype(BF16)
     combine = picks.T[:owned].astype(BF16)
     combine = jnp.concatenate([combine, combine], axis=1)
-    for k in range(LM):
-        high, low = split(parts[pl.ds(k * SLOTP, devices), :SHELLS])
-        both = jnp.concatenate([high, low], axis=0).astype(BF16)
-        acc[k * owned : (k + 1) * owned, :SHELLS] = dot(combine, both)
+    left = lax.broadcasted_iota(jnp.int32, (owned, 128), 1) < SHELLS
+    for k in range(HALF + 1):
+        high, low = split(parts[k * SLOTP : k * SLOTP + devices, :])
+        both = dot(combine, jnp.concatenate([high, low], axis=0).astype(BF16))
+        other = pltpu.roll(both, SHELLS, 1)
+        at_k = (k if k < HALF else LM - 1) * owned
+        acc[at_k : at_k + owned, :] = jnp.where(left, both, other)
+        if k < HALF:
+            at_k += HALF * owned
+            acc[at_k : at_k + owned, :] = jnp.where(left, other, both)
 
     for d in range(LMAX + 1):
         begin, end = d * d, (d + 1) * (d + 1)
-        high, low = split(acc[begin * owned : end * owned, :SHELLS])
-        high, low = high.astype(BF16), low.astype(BF16)
-        table = dot(high, ghigh[d]) + dot(low, ghigh[d]) + dot(high, glow[d])
-        thigh, tlow = split(table)
-        lane_rank = lax.broadcasted_iota(jnp.int32, table.shape, 1)
-        table = jnp.where(lane_rank < SHELLS, thigh, tlow).astype(BF16)
-        for k in range(begin, end, 2):
-            rows = [
-                table[(n - begin) * owned : (n - begin + 1) * owned]
-                for n in range(k, min(k + 2, end))
-            ]
-            picked = dot(gather, jnp.concatenate(rows, axis=1))
-            for n in range(len(rows)):
-                at_k = (k + n) * SLOTP
-                tables[at_k : at_k + devices, :] = picked[:, n * 128 : (n + 1) * 128]
-    for k in range(LM, KP):
-        tables[k * SLOTP : k * SLOTP + devices, :] = jnp.zeros((devices, 128), F32)
+        twice = acc[begin * owned : end * owned, :]
+        high, low = split(twice)
+        wide = lax.broadcasted_iota(jnp.int32, twice.shape, 1) < SHELLS
+        both = dot(jnp.where(wide, high, low).astype(BF16), green[d])
+        thigh, tlow = split(both[:, :128] + both[:, 128:])
+        small[begin * owned : end * owned, :] = jnp.where(wide, thigh, tlow).astype(BF16)
+    for k in range(0, LM, 2):
+        many = min(2, LM - k)
+        rows = [small[n * owned : (n + 1) * owned, :] for n in range(k, k + many)]
+        picked = dot(gather, jnp.concatenate(rows, axis=1))
+        for n in range(many):
+            at_k = (k + n) * SLOTP
+            tables[at_k : at_k + devices, :] = picked[:, n * 128 : (n + 1) * 128]
 
     def evaluate(i):
         table = tables[pl.ds(i, KP, stride=SLOTP), :].astype(BF16)
@@ -349,20 +373,17 @@
                 device_id_type=MESH,
             ).start()
 
-    cuts = (0, 16, 32, 64, 96, devices)
-    for n in range(len(cuts) - 1):
-        for i in range(cuts[n], cuts[n + 1]):
+    pairs = LM // 2
+    for g in range(devices // WAVE):
+        for i in range(g * WAVE, (g + 1) * WAVE):
             evaluate(i)
-        if n:
-            answer(cuts[n - 1], cuts[n])
+        for n in range(g * WAVE * pairs // devices, (g + 1) * WAVE * pairs // devices):
+            first = acc[2 * n * owned : (2 * n + 1) * owned, :]
+            second = acc[(2 * n + 1) * owned : (2 * n + 2) * owned, :]
+            sums[:, n * 128 : (n + 1) * 128] = jnp.where(left, first, second)
+        answer(g * WAVE, (g + 1) * WAVE)
     back[0] = reply[0]
-    answer(cuts[-2], cuts[-1])
-    for k in range(0, LM, 2):
-        first = acc[k * owned : (k + 1) * owned, :SHELLS]
-        if k + 1 < LM:
-            second = acc[(k + 1) * owned : (k + 2) * owned, :SHELLS]
-            first = jnp.concatenate([first, second], axis=1)
-        sums[:, k * SHELLS : min(k + 2, LM) * SHELLS] = first
+    sums[:, pairs * 128 :] = acc[(LM - 1) * owned : LM * owned, :SHELLS]
 
     everything = pltpu.make_async_remote_copy(
         src_ref=piece(pay, 1, devices - 1),
@@ -385,7 +406,9 @@
     answers.wait_recv()
 
 
-def finish_kernel(mine, back, sums, potential, moments):
+def finish_kernel(mine, back, sums, potential, moments, sem):
+    whole = pltpu.make_async_copy(sums, moments, sem)
+    whole.start()
     batches = potential.shape[0]
     chosen = mine[...].astype(BF16)
     for h in range(2):
@@ -397,7 +420,7 @@
             + dot(chosen, low.astype(BF16))
         )
         potential[:, h * 128 : (h + 1) * 128] = total[:batches]
-    moments[...] = sums[...]
+    whole.wait()
 
 
 VMEM = pl.BlockSpec(memory_space=pltpu.VMEM)
@@ -421,7 +444,7 @@
     owned = owner_slot.shape[0] // devices
     spaces = batches * slots
     sds = jax.ShapeDtypeStruct
-    ghigh, glow = green_pair()
+    green_table = green_blocks()
     sums, mine, back = pl.pallas_call(
         fused_kernel,
         out_shape=(
@@ -429,7 +452,7 @@
             sds((8, devices), F32),
             sds((devices, 2, 128), F32),
         ),
-        in_specs=[SMEM] + [HBM] * 10,
+        in_specs=[SMEM] + [HBM] * 9,
         out_specs=(VMEM, VMEM, VMEM),
         scratch_shapes=[
             pltpu.SMEM((batches, slots), jnp.int32),
@@ -439,8 +462,7 @@
             pltpu.VMEM((3, batches, points), F32),
             pltpu.VMEM((batches, points), F32),
             pltpu.VMEM((batches, slots, points), jnp.int32),
-            pltpu.VMEM(ghigh.shape, BF16),
-            pltpu.VMEM(glow.shape, BF16),
+            pltpu.VMEM(green_table.shape, BF16),
             pltpu.VMEM((4, devices), jnp.int32),
             pltpu.VMEM((4, spaces, 128), F32),
             pltpu.VMEM((ROWS, spaces, 128), F32),
@@ -449,11 +471,12 @@
             pltpu.VMEM((2, devices * KP, 128), F32),
             pltpu.VMEM((2, devices, 128), F32),
             pltpu.VMEM((devices, SHELLS, 256), BF16),
-            pltpu.VMEM((KP * SLOTP, 128), F32),
+            pltpu.VMEM(((HALF + 1) * SLOTP, 128), F32),
             pltpu.VMEM((LM * owned, 128), F32),
+            pltpu.VMEM((LM * owned, 128), BF16),
             pltpu.VMEM((KP * SLOTP, 128), F32),
             pltpu.VMEM((devices, 2, 128), F32),
-            pltpu.SemaphoreType.DMA((10,)),
+            pltpu.SemaphoreType.DMA((9,)),
             pltpu.SemaphoreType.DMA,
             pltpu.SemaphoreType.DMA((devices // WAVE,)),
             pltpu.SemaphoreType.DMA,
@@ -475,8 +498,7 @@
                 jnp.transpose(point_coords, (1, 0, 2)),
                 charge,
                 shell_index,
-                jnp.asarray(ghigh),
-                jnp.asarray(glow),
+                jnp.asarray(green_table),
                 jnp.asarray(np.array(ORDER, dtype=np.int32).T),
             )
         ]
@@ -485,7 +507,8 @@
         finish_kernel,
         out_shape=(sds(charge.shape, F32), sds(sums.shape, F32)),
         in_specs=[VMEM] * 3,
-        out_specs=(VMEM, VMEM),
+        out_specs=(VMEM, HBM),
+        scratch_shapes=[pltpu.SemaphoreType.DMA],
         compiler_params=pltpu.CompilerParams(vmem_limit_bytes=4 << 20),
         name="finish",
     )(mine, back, sums)

time: 36.7 us -> 35.4 us (0.965)
  Pallas kernels: 35.3 us -> 33.9 us
    pallas_call x1, Pallas kernels: 33.9 us -> 32.5 us  [body(): pl.pallas_call(fused_kernel, out_shape=(sds((owned, LM * SHELLS), F32), s...]
where the time goes in v5:
time: 35.4 us; the launch traced here: 35.2 us
  Pallas kernels  33.9 us (96%)
  between operations  1.29 us (4%)
    pallas_call x1, Pallas kernels, body(): pl.pallas_call(fused_kernel, out_shape=(sds((owned, LM * SHELLS), F32), s...  32.5 us
    pallas_call x1, Pallas kernels, body(): pl.pallas_call(finish_kernel, out_shape=(sds(charge.shape, F32), sds(sums...  1.37 us

profile of v5, /device:TPU:1, one launch (start us, length us, event | category | flops | bytes accessed | tf_op | source)
XLA Modules:
  0.0 35.2 jit_solution(10717956390860802968)
XLA Ops:
  1.3 32.5 %fused.1 = (f32[32,3136]{1,0:T(8,128)S(1)}, f32[8,128]{1,0:T(8,128)S(1)}, f32[128,2,128]{2,1,0:T(2,128)S(1)}) custom-call(s32[1]{0:T(128)S(6)} %copy.12.refs_0_, s32[4,32]{1,0:T(4,128)} %refs_1_.1, s32[4]{0:T(128)} %refs_2_.1, s32[4096]{0:T(1024)} %refs_3_.1, f32[3,4096]{1,0:T(4,128)} %refs_4_.1, f32[3,4,256]{2,1,0:T(4,128)} %bitcast.1, f32[4,256]{1,0:T(4,128)} %refs_6_.1, ...), custom_call_target="tpu_custom_call" | custom-call | tf_op jit(solution)/shard_map/fused/pallas_call | solution.py:448
  33.8 1.4 %finish.1 = (f32[4,256]{1,0:T(4,128)}, f32[32,3136]{1,0:T(8,128)}) custom-call(f32[8,128]{1,0:T(8,128)S(1)} %get-tuple-element.5.mine, f32[128,2,128]{2,1,0:T(2,128)S(1)} %get-tuple-element.6.back, f32[32,3136]{1,0:T(8,128)S(1)} %get-tuple-element.7.sums), custom_call_target="tpu_custom_call" | custom-call | tf_op jit(solution)/shard_map/finish/pallas_call | solution.py:506

commit v6 on v5

--- a/solution.py
+++ b/solution.py
@@ -8,7 +8,7 @@
 from jax.experimental.pallas import tpu as pltpu
 from jax.sharding import PartitionSpec as P
 
-MESH = pl.DeviceIdType.MESH
+LOGICAL = pl.DeviceIdType.LOGICAL
 F32 = jnp.float32
 BF16 = jnp.bfloat16
 SHELLS = 64
@@ -16,8 +16,9 @@
 LM = 49
 KP = 56
 HALF = 24
+LANES = 8
 SOFTEN = 0.01
-ROWS = 11
+ROWS = 10
 PITCH = 16
 SLOTP = 136
 WAVE = 32
@@ -128,11 +129,15 @@
         small,
         tables,
         reply,
+        names,
+        called,
         load_sem,
         send_sem,
         recv_sem,
         reply_send,
         reply_recv,
+        name_send,
+        name_recv,
     ) = refs
     labels, count, owner, atoms, coords, charge, shell, green, steps = held
     loads = [
@@ -147,23 +152,26 @@
     owned = sums.shape[0]
     gy = lax.axis_index("gy")
     at = (lax.axis_index("gx"), gy // 8, lax.rem(gy, 8) // 2, lax.rem(gy, 2))
-    spans = (4, 4, 4, 2)
+    spans, scales = (4, 4, 4, 2), (32, 8, 2, 1)
     moved_to = [
-        [lax.rem(at[axis] + step, spans[axis]) for step in range(spans[axis])]
+        [lax.rem(at[axis] + step, spans[axis]) * scales[axis] for step in range(spans[axis])]
         for axis in range(4)
     ]
+    planes = {
+        (dy, dz): moved_to[0][dy] + moved_to[1][dz] for dy in range(4) for dz in range(4)
+    }
+    lines = {
+        (dx, dc): moved_to[2][dx] + moved_to[3][dc] for dx in range(4) for dc in range(2)
+    }
 
     def peer(i, sign):
-        y, z, x, c = [
-            moved_to[axis][sign * step % spans[axis]]
-            for axis, step in enumerate(ORDER[i])
-        ]
-        return (y, z * 8 + x * 2 + c)
+        dy, dz, dx, dc = [sign * d % span for d, span in zip(ORDER[i], spans)]
+        return planes[dy, dz] + lines[dx, dc]
 
     barrier = pltpu.get_barrier_semaphore()
     for i in range(1, devices):
         pl.semaphore_signal(
-            barrier, inc=1, device_id=peer(i, -1), device_id_type=MESH
+            barrier, inc=1, device_id=peer(i, -1), device_id_type=LOGICAL
         )
 
     top = jnp.where(
@@ -228,7 +236,7 @@
     goes = (place[3] == row_of.astype(F32)).astype(F32)
     goes = goes.T.astype(BF16)
     flat_pay = pay.reshape(devices * PITCH, 128)
-    for r in range(ROWS):
+    for r in range(ROWS + 1):
         high, rest = split(src[r])
         moved = dot(goes, high.astype(BF16))
         if r not in (6, 7, 10):
@@ -236,7 +244,10 @@
             moved = (
                 moved + dot(goes, middle.astype(BF16)) + dot(goes, low.astype(BF16))
             )
-        flat_pay[pl.ds(r, devices, stride=PITCH), :] = moved
+        if r < ROWS:
+            flat_pay[pl.ds(r, devices, stride=PITCH), :] = moved
+        else:
+            names[...] = moved[:, :LANES]
     lives = dot(goes, jnp.concatenate(lives, axis=0).astype(BF16))
     mine[...] = lives.T[:8]
 
@@ -252,9 +263,23 @@
             send_sem=send_sem,
             recv_sem=recv_sem.at[i // WAVE],
             device_id=peer(i, 1),
-            device_id_type=MESH,
+            device_id_type=LOGICAL,
         ).start()
 
+    def called_by(i, size):
+        return names.at[pl.ds(i, size)], called.at[pl.ds(i, size)]
+
+    for i in range(1, devices):
+        here_name, there_name = called_by(i, 1)
+        pltpu.make_async_remote_copy(
+            src_ref=here_name,
+            dst_ref=there_name,
+            send_sem=name_send,
+            recv_sem=name_recv,
+            device_id=peer(i, 1),
+            device_id_type=LOGICAL,
+        ).start()
+    called[0:1, :] = names[0:1, :]
     arrived[0] = pay[0]
     flat = arrived.reshape(devices * PITCH, 128)
     shell_rank = lax.broadcasted_iota(jnp.int32, (SHELLS, 128), 0).astype(F32)
@@ -297,8 +322,8 @@
             dst_ref=piece(arrived, 1, size),
             send_sem=send_sem,
             recv_sem=recv_sem.at[g],
-            device_id=(0, 0),
-            device_id_type=MESH,
+            device_id=0,
+            device_id_type=LOGICAL,
         ).wait_recv()
 
     @pl.loop(0, devices // WAVE)
@@ -317,7 +342,18 @@
         for e in range(WAVE):
             forward(g * WAVE + e)
 
-    marks = flat[pl.ds(10, devices, stride=PITCH), :]
+    here_names, there_names = called_by(1, devices - 1)
+    called_all = pltpu.make_async_remote_copy(
+        src_ref=here_names,
+        dst_ref=there_names,
+        send_sem=name_send,
+        recv_sem=name_recv,
+        device_id=0,
+        device_id_type=LOGICAL,
+    )
+    called_all.wait_send()
+    called_all.wait_recv()
+    marks = jnp.broadcast_to(called[:, :1], (devices, 128))
     picks = (
         marks == lax.broadcasted_iota(jnp.int32, (devices, 128), 1).astype(F32)
     ).astype(F32)
@@ -370,7 +406,7 @@
                 send_sem=reply_send,
                 recv_sem=reply_recv,
                 device_id=peer(i, -1),
-                device_id_type=MESH,
+                device_id_type=LOGICAL,
             ).start()
 
     pairs = LM // 2
@@ -390,8 +426,8 @@
         dst_ref=piece(arrived, 1, devices - 1),
         send_sem=send_sem,
         recv_sem=recv_sem.at[0],
-        device_id=(0, 0),
-        device_id_type=MESH,
+        device_id=0,
+        device_id_type=LOGICAL,
     )
     everything.wait_send()
     answers = pltpu.make_async_remote_copy(
@@ -399,8 +435,8 @@
         dst_ref=back.at[pl.ds(1, devices - 1)],
         send_sem=reply_send,
         recv_sem=reply_recv,
-        device_id=(0, 0),
-        device_id_type=MESH,
+        device_id=0,
+        device_id_type=LOGICAL,
     )
     answers.wait_send()
     answers.wait_recv()
@@ -465,7 +501,7 @@
             pltpu.VMEM(green_table.shape, BF16),
             pltpu.VMEM((4, devices), jnp.int32),
             pltpu.VMEM((4, spaces, 128), F32),
-            pltpu.VMEM((ROWS, spaces, 128), F32),
+            pltpu.VMEM((ROWS + 1, spaces, 128), F32),
             pltpu.VMEM((devices, PITCH, 128), F32),
             pltpu.VMEM((devices, PITCH, 128), F32),
             pltpu.VMEM((2, devices * KP, 128), F32),
@@ -476,9 +512,13 @@
             pltpu.VMEM((LM * owned, 128), BF16),
             pltpu.VMEM((KP * SLOTP, 128), F32),
             pltpu.VMEM((devices, 2, 128), F32),
+            pltpu.VMEM((devices, LANES), F32),
+            pltpu.VMEM((devices, LANES), F32),
             pltpu.SemaphoreType.DMA((9,)),
             pltpu.SemaphoreType.DMA,
             pltpu.SemaphoreType.DMA((devices // WAVE,)),
+            pltpu.SemaphoreType.DMA,
+            pltpu.SemaphoreType.DMA,
             pltpu.SemaphoreType.DMA,
             pltpu.SemaphoreType.DMA,
         ],

time: 35.4 us -> 34.9 us (0.986)
  Pallas kernels: 33.9 us -> 33.4 us
    pallas_call x1, Pallas kernels: 32.5 us -> 32.1 us  [body(): pl.pallas_call(fused_kernel, out_shape=(sds((owned, LM * SHELLS), F32), s...]
where the time goes in v6:
time: 34.9 us; the launch traced here: 34.7 us
  Pallas kernels  33.4 us (96%)
  between operations  1.29 us (4%)
    pallas_call x1, Pallas kernels, body(): pl.pallas_call(fused_kernel, out_shape=(sds((owned, LM * SHELLS), F32), s...  32.1 us
    pallas_call x1, Pallas kernels, body(): pl.pallas_call(finish_kernel, out_shape=(sds(charge.shape, F32), sds(sums...  1.37 us

profile of v6, /device:TPU:1, one launch (start us, length us, event | category | flops | bytes accessed | tf_op | source)
XLA Modules:
  0.0 34.7 jit_solution(4538593746507740592)
XLA Ops:
  1.3 32.1 %fused.1 = (f32[32,3136]{1,0:T(8,128)S(1)}, f32[8,128]{1,0:T(8,128)S(1)}, f32[128,2,128]{2,1,0:T(2,128)S(1)}) custom-call(s32[1]{0:T(128)S(6)} %copy.12.refs_0_, s32[4,32]{1,0:T(4,128)} %refs_1_.1, s32[4]{0:T(128)} %refs_2_.1, s32[4096]{0:T(1024)} %refs_3_.1, f32[3,4096]{1,0:T(4,128)} %refs_4_.1, f32[3,4,256]{2,1,0:T(4,128)} %bitcast.1, f32[4,256]{1,0:T(4,128)} %refs_6_.1, ...), custom_call_target="tpu_custom_call" | custom-call | tf_op jit(solution)/shard_map/fused/pallas_call | solution.py:484
  33.4 1.4 %finish.1 = (f32[4,256]{1,0:T(4,128)}, f32[32,3136]{1,0:T(8,128)}) custom-call(f32[8,128]{1,0:T(8,128)S(1)} %get-tuple-element.5.mine, f32[128,2,128]{2,1,0:T(2,128)S(1)} %get-tuple-element.6.back, f32[32,3136]{1,0:T(8,128)S(1)} %get-tuple-element.7.sums), custom_call_target="tpu_custom_call" | custom-call | tf_op jit(solution)/shard_map/finish/pallas_call | solution.py:546

commit v7 on v6

--- a/solution.py
+++ b/solution.py
@@ -148,7 +148,7 @@
         one.start()
     batches, slots = labels.shape
     spaces = batches * slots
-    devices = pay.shape[0]
+    devices = back.shape[0]
     owned = sums.shape[0]
     gy = lax.axis_index("gy")
     at = (lax.axis_index("gx"), gy // 8, lax.rem(gy, 8) // 2, lax.rem(gy, 2))
@@ -188,7 +188,7 @@
 
     for k in range(LM, KP):
         tables[k * SLOTP : k * SLOTP + devices, :] = jnp.zeros((devices, 128), F32)
-    parts[(HALF * SLOTP) :, :] = jnp.zeros((SLOTP, 128), F32)
+    parts[HALF * SLOTP : (HALF + 1) * SLOTP, :] = jnp.zeros((SLOTP, 128), F32)
 
     for one in loads:
         one.wait()
@@ -233,11 +233,11 @@
     for axis in range(4):
         there = lax.rem(steps[axis : axis + 1, :] + at[axis], spans[axis])
         row_of = row_of * spans[axis] + there
-    goes = (place[3] == row_of.astype(F32)).astype(F32)
+    goes = (place[3, :spaces] == row_of.astype(F32)).astype(F32)
     goes = goes.T.astype(BF16)
-    flat_pay = pay.reshape(devices * PITCH, 128)
+    flat_pay = pay.reshape((devices + 1) * PITCH, 128)
     for r in range(ROWS + 1):
-        high, rest = split(src[r])
+        high, rest = split(src[r, :spaces])
         moved = dot(goes, high.astype(BF16))
         if r not in (6, 7, 10):
             middle, low = split(rest)
@@ -281,7 +281,7 @@
         ).start()
     called[0:1, :] = names[0:1, :]
     arrived[0] = pay[0]
-    flat = arrived.reshape(devices * PITCH, 128)
+    flat = arrived.reshape((devices + 1) * PITCH, 128)
     shell_rank = lax.broadcasted_iota(jnp.int32, (SHELLS, 128), 0).astype(F32)
 
     def shapes(g):
@@ -500,18 +500,18 @@
             pltpu.VMEM((batches, slots, points), jnp.int32),
             pltpu.VMEM(green_table.shape, BF16),
             pltpu.VMEM((4, devices), jnp.int32),
-            pltpu.VMEM((4, spaces, 128), F32),
-            pltpu.VMEM((ROWS + 1, spaces, 128), F32),
-            pltpu.VMEM((devices, PITCH, 128), F32),
-            pltpu.VMEM((devices, PITCH, 128), F32),
-            pltpu.VMEM((2, devices * KP, 128), F32),
-            pltpu.VMEM((2, devices, 128), F32),
+            pltpu.VMEM((4, spaces + 8, 128), F32),
+            pltpu.VMEM((ROWS + 1, spaces + 8, 128), F32),
+            pltpu.VMEM((devices + 1, PITCH, 128), F32),
+            pltpu.VMEM((devices + 1, PITCH, 128), F32),
+            pltpu.VMEM((2, (devices + 1) * KP, 128), F32),
+            pltpu.VMEM((2, devices + 8, 128), F32),
             pltpu.VMEM((devices, SHELLS, 256), BF16),
-            pltpu.VMEM(((HALF + 1) * SLOTP, 128), F32),
+            pltpu.VMEM(((HALF + 2) * SLOTP, 128), F32),
             pltpu.VMEM((LM * owned, 128), F32),
             pltpu.VMEM((LM * owned, 128), BF16),
-            pltpu.VMEM((KP * SLOTP, 128), F32),
-            pltpu.VMEM((devices, 2, 128), F32),
+            pltpu.VMEM(((KP + 1) * SLOTP, 128), F32),
+            pltpu.VMEM((devices + 8, 2, 128), F32),
             pltpu.VMEM((devices, LANES), F32),
             pltpu.VMEM((devices, LANES), F32),
             pltpu.SemaphoreType.DMA((9,)),

time: 34.9 us -> 35 us (level)
  no operation moved by 1% of the time
where the time goes in v7:
time: 35 us; the launch traced here: 34.8 us
  Pallas kernels  33.5 us (96%)
  between operations  1.29 us (4%)
    pallas_call x1, Pallas kernels, body(): pl.pallas_call(fused_kernel, out_shape=(sds((owned, LM * SHELLS), F32), s...  32.1 us
    pallas_call x1, Pallas kernels, body(): pl.pallas_call(finish_kernel, out_shape=(sds(charge.shape, F32), sds(sums...  1.37 us

profile of v7, /device:TPU:1, one launch (start us, length us, event | category | flops | bytes accessed | tf_op | source)
XLA Modules:
  0.0 34.8 jit_solution(5090715482618808595)
XLA Ops:
  1.3 32.1 %fused.1 = (f32[32,3136]{1,0:T(8,128)S(1)}, f32[8,128]{1,0:T(8,128)S(1)}, f32[128,2,128]{2,1,0:T(2,128)S(1)}) custom-call(s32[1]{0:T(128)S(6)} %copy.12.refs_0_, s32[4,32]{1,0:T(4,128)} %refs_1_.1, s32[4]{0:T(128)} %refs_2_.1, s32[4096]{0:T(1024)} %refs_3_.1, f32[3,4096]{1,0:T(4,128)} %refs_4_.1, f32[3,4,256]{2,1,0:T(4,128)} %bitcast.1, f32[4,256]{1,0:T(4,128)} %refs_6_.1, ...), custom_call_target="tpu_custom_call" | custom-call | tf_op jit(solution)/shard_map/fused/pallas_call | solution.py:484
  33.4 1.4 %finish.1 = (f32[4,256]{1,0:T(4,128)}, f32[32,3136]{1,0:T(8,128)}) custom-call(f32[8,128]{1,0:T(8,128)S(1)} %get-tuple-element.5.mine, f32[128,2,128]{2,1,0:T(2,128)S(1)} %get-tuple-element.6.back, f32[32,3136]{1,0:T(8,128)S(1)} %get-tuple-element.7.sums), custom_call_target="tpu_custom_call" | custom-call | tf_op jit(solution)/shard_map/finish/pallas_call | solution.py:546

commit v8 on v6

--- a/solution.py
+++ b/solution.py
@@ -123,7 +123,6 @@
         arrived,
         ys,
         ws,
-        hots,
         parts,
         acc,
         small,
@@ -308,7 +307,6 @@
             shells = flat[pl.ds(i * PITCH + 6 + h, 1), :]
             hot.append((shells == shell_rank).astype(F32).astype(BF16))
         hot = jnp.concatenate(hot, axis=1)
-        hots[i] = hot
         both = dot(jnp.concatenate(stack, axis=1), hot, ((1,), (1,)))
         part = both[:KP] + both[KP:]
         parts[pl.ds(i, HALF, stride=SLOTP), :] = jnp.concatenate(
@@ -389,7 +387,13 @@
 
     def evaluate(i):
         table = tables[pl.ds(i, KP, stride=SLOTP), :].astype(BF16)
-        hot = hots[i]
+        hot = jnp.concatenate(
+            [
+                (flat[pl.ds(i * PITCH + 6 + h, 1), :] == shell_rank).astype(F32).astype(BF16)
+                for h in range(2)
+            ],
+            axis=1,
+        )
         picked = dot(table, jnp.concatenate([hot, hot], axis=0))
         for h in range(2):
             y = ys[h, pl.ds(pl.multiple_of(i * KP, 8), KP), :]
@@ -506,7 +510,6 @@
             pltpu.VMEM((devices, PITCH, 128), F32),
             pltpu.VMEM((2, devices * KP, 128), F32),
             pltpu.VMEM((2, devices, 128), F32),
-            pltpu.VMEM((devices, SHELLS, 256), BF16),
             pltpu.VMEM(((HALF + 1) * SLOTP, 128), F32),
             pltpu.VMEM((LM * owned, 128), F32),
             pltpu.VMEM((LM * owned, 128), BF16),

time: 34.9 us -> 35.1 us (level)
  no operation moved by 1% of the time
where the time goes in v8:
time: 35.1 us; the launch traced here: 34.9 us
  Pallas kernels  33.6 us (96%)
  between operations  1.29 us (4%)
    pallas_call x1, Pallas kernels, body(): pl.pallas_call(fused_kernel, out_shape=(sds((owned, LM * SHELLS), F32), s...  32.2 us
    pallas_call x1, Pallas kernels, body(): pl.pallas_call(finish_kernel, out_shape=(sds(charge.shape, F32), sds(sums...  1.37 us

profile of v8, /device:TPU:1, one launch (start us, length us, event | category | flops | bytes accessed | tf_op | source)
XLA Modules:
  0.0 34.9 jit_solution(11166622615776709517)
XLA Ops:
  1.3 32.2 %fused.1 = (f32[32,3136]{1,0:T(8,128)S(1)}, f32[8,128]{1,0:T(8,128)S(1)}, f32[128,2,128]{2,1,0:T(2,128)S(1)}) custom-call(s32[1]{0:T(128)S(6)} %copy.12.refs_0_, s32[4,32]{1,0:T(4,128)} %refs_1_.1, s32[4]{0:T(128)} %refs_2_.1, s32[4096]{0:T(1024)} %refs_3_.1, f32[3,4096]{1,0:T(4,128)} %refs_4_.1, f32[3,4,256]{2,1,0:T(4,128)} %bitcast.1, f32[4,256]{1,0:T(4,128)} %refs_6_.1, ...), custom_call_target="tpu_custom_call" | custom-call | tf_op jit(solution)/shard_map/fused/pallas_call | solution.py:488
  33.5 1.4 %finish.1 = (f32[4,256]{1,0:T(4,128)}, f32[32,3136]{1,0:T(8,128)}) custom-call(f32[8,128]{1,0:T(8,128)S(1)} %get-tuple-element.5.mine, f32[128,2,128]{2,1,0:T(2,128)S(1)} %get-tuple-element.6.back, f32[32,3136]{1,0:T(8,128)S(1)} %get-tuple-element.7.sums), custom_call_target="tpu_custom_call" | custom-call | tf_op jit(solution)/shard_map/finish/pallas_call | solution.py:549
